TPU v7x, 128 devices: a whole 4x4x4 slice. The times are simulated.
128 devices in a mesh: rep: 1, dp: 128 (over x, y, z, core).
Axes of the slice: x: 4, y: 4, z: 4, core: 2. Of those that a mesh axis runs over, the one named last changes fastest.
Arguments:
- x: bfloat16 [128, 2048, 1024], P(('rep', 'dp'))
- dy: bfloat16 [128, 2048, 1024], P(('rep', 'dp'))
- w_gate: bfloat16 [2, 1024, 2560], P(None, 'dp')
- w_up: bfloat16 [2, 1024, 2560], P(None, 'dp')
- w_down: bfloat16 [2, 2560, 1024], P(None, 'dp')
Outputs:
- output 1: bfloat16 [128, 2048, 1024], P(('rep', 'dp'))
- output 2: bfloat16 [2, 1024, 2560], P('rep', 'dp')
- output 3: bfloat16 [2, 1024, 2560], P('rep', 'dp')
- output 4: bfloat16 [2, 2560, 1024], P('rep', 'dp')
All inputs are finite; a program needn't handle non-finite values.
Results may differ from a plain program's by a relative error of at most 0.018.
Values are sent between devices in bfloat16 or wider.
A program may use at most 1.5 GiB of HBM per device.

v0:
```python
import jax
import jax.numpy as jnp
from jax import lax

NAMES = ("w_gate", "w_up", "w_down")


def matmul(a, w):
    return jnp.dot(a, w, preferred_element_type=jnp.float32).astype(jnp.bfloat16)


def normed(h):
    wide = h.astype(jnp.float32)
    scale = lax.rsqrt(jnp.mean(wide**2, -1, keepdims=True) + 1e-6)
    return (wide * scale).astype(jnp.bfloat16)


def layer(h, w):
    a = normed(h)
    gate = jnp.dot(a, w["w_gate"], preferred_element_type=jnp.float32)
    up = jnp.dot(a, w["w_up"], preferred_element_type=jnp.float32)
    return h + matmul((jax.nn.silu(gate) * up).astype(jnp.bfloat16), w["w_down"])


def stack(weights, h):
    for number in range(weights["w_gate"].shape[0]):
        h = layer(h, {name: w[number] for name, w in weights.items()})
    return h


def solution(mesh):
    groups = mesh.shape["rep"]

    def step(x, dy, *weights):
        shape = x.shape
        x, dy = (t.reshape(groups, -1, *t.shape[1:]) for t in (x, dy))

        def of_a_group(x, dy):
            _, back = jax.vjp(stack, dict(zip(NAMES, weights, strict=True)), x)
            by_weights, by_x = back(dy)
            return (by_x, *(by_weights[name] for name in NAMES))

        by_x, *by_weights = jax.vmap(of_a_group)(x, dy)
        return (by_x.reshape(shape), *(t.reshape(-1, *t.shape[2:]) for t in by_weights))

    return step
```

profile of v0, /device:TPU:0, one launch (start us, length us, event | category | flops | bytes accessed | tf_op | source)
XLA Modules:
  0.0 3074.3 jit_solution(4966516667698633444)
XLA Ops:
  30.4 50.7 %all-gather.29.cloned.1.call-done = bf16[1,1024,2560]{2,1,0:T(8,128)(2,1)} async-done(((bf16[1,8,2560]{2,1,0:T(8,128)(2,1)}), bf16[1,1024,2560]{2,1,0:T(8,128)(2,1)}) %all-gather.29.cloned.1.call-update) | async-done | bytes 5242896 | tf_op jit(solution)/vmap(jvp())/squeeze | solution.py:27
  81.1 18.4 fusion.61
  99.5 49.8 %all-gather.31.cloned.1.call-done = bf16[1,1024,2560]{2,1,0:T(8,128)(2,1)} async-done(((bf16[1,8,2560]{2,1,0:T(8,128)(2,1)}), bf16[1,1024,2560]{2,1,0:T(8,128)(2,1)}) %all-gather.31.cloned.1.call-update) | async-done | bytes 5242896 | tf_op jit(solution)/vmap(jvp())/squeeze | solution.py:27
  149.3 18.6 fusion.57
  168.0 15.3 fusion.26
  183.2 38.4 %all-gather.33.cloned.1.call-done = bf16[1,2560,1024]{2,0,1:T(2,128)(2,1)} async-done(((bf16[1,20,1024]{2,0,1:T(2,128)(2,1)}), bf16[1,2560,1024]{2,0,1:T(2,128)(2,1)}) %all-gather.33.cloned.1.call-update) | async-done | bytes 5242896 | tf_op jit(solution)/vmap(jvp())/squeeze | solution.py:27
  221.6 20.9 fusion.41
  243.1 51.3 %all-gather.37.cloned.1.call-done = bf16[1,2560,1024]{2,0,1:T(2,128)(2,1)} async-done(((bf16[1,20,1024]{2,0,1:T(2,128)(2,1)}), bf16[1,2560,1024]{2,0,1:T(2,128)(2,1)}) %all-gather.37.cloned.1.call-update) | async-done | bytes 5242896 | tf_op jit(solution)/vmap(jvp())/squeeze | solution.py:27
  294.4 18.3 convolution_convert_fusion.1
  312.7 50.3 %all-gather.35.cloned.1.call-done = bf16[1,1024,2560]{2,1,0:T(8,128)(2,1)} async-done(((bf16[1,8,2560]{2,1,0:T(8,128)(2,1)}), bf16[1,1024,2560]{2,1,0:T(8,128)(2,1)}) %all-gather.35.cloned.1.call-update) | async-done | bytes 5242896 | tf_op jit(solution)/vmap(jvp())/squeeze | solution.py:27
  363.0 18.4 fusion.54
  381.5 20.9 fusion.22
  402.4 29.3 all-gather.39.cloned.1.call-done
  431.7 14.6 fusion.49
  453.3 18.2 fusion.6
  471.5 20.0 fusion.24
  491.5 17.5 fusion.43
  514.3 18.5 convolution_convert_fusion
  532.8 20.7 fusion.18
  553.6 18.5 fusion.9
  575.9 13.6 fusion.79
  589.6 17.6 fusion.84
  607.2 22.6 fusion.28
  629.8 17.8 fusion.67
  647.7 369.8 %fusion.97 = (f32[1024,24]{0,1:T(8,128)S(1)}, f32[24,1024]{1,0:T(8,128)S(1)}) fusion(f32[1024,2560]{0,1:T(8,128)} %fusion.67, f32[2560,1024]{1,0:T(8,128)} %fusion.28), kind=kCustom, calls=%all-reduce-scatter.2 | all-reduce-scatter fusion | flops 6291457 | bytes 21168128
  1029.3 9.2 collective-permute-start.8
  1045.0 16.7 collective-permute-start.12
  1101.6 20.1 fusion.20
  1135.0 17.4 fusion.40
  1193.1 560.1 %reduce-scatter.25.cloned.1.call-done = f32[2560,8]{0,1:T(8,128)} async-done(((f32[2560,1024]{0,1:T(8,128)}), f32[2560,8]{0,1:T(8,128)}) %reduce-scatter.25.cloned.1.call-update) | async-done | bytes 81936
  1754.8 654.8 %reduce-scatter.21.cloned.1.call-done = f32[2560,8]{0,1:T(8,128)} async-done(((f32[2560,1024]{0,1:T(8,128)}), f32[2560,8]{0,1:T(8,128)}) %reduce-scatter.21.cloned.1.call-update) | async-done | bytes 81936
  2410.5 655.2 %reduce-scatter.19.cloned.1.call-done = f32[2560,8]{0,1:T(8,128)} async-done(((f32[2560,1024]{0,1:T(8,128)}), f32[2560,8]{0,1:T(8,128)}) %reduce-scatter.19.cloned.1.call-update) | async-done | bytes 81936
  (170 shorter events, 155.4 us)
Async XLA Ops:
  7.2 74.0 %all-gather.29.cloned.1.call-start = ((), (), s32[]{:S(2)}) async-start(), calls=%async_computation.4 | async-start | bytes 5283840 | tf_op jit(solution)/vmap(jvp())/squeeze | solution.py:27
  8.7 140.7 %all-gather.31.cloned.1.call-start = ((), (), s32[]{:S(2)}) async-start(), calls=%async_computation.5 | async-start | bytes 5283840 | tf_op jit(solution)/vmap(jvp())/squeeze | solution.py:27
  10.2 211.5 %all-gather.33.cloned.1.call-start = ((), (), s32[]{:S(2)}) async-start(), calls=%async_computation.6 | async-start | bytes 10567680 | tf_op jit(solution)/vmap(jvp())/squeeze | solution.py:27
  12.0 282.4 %all-gather.37.cloned.1.call-start = ((), (), s32[]{:S(2)}) async-start(), calls=%async_computation.8 | async-start | bytes 10567680 | tf_op jit(solution)/vmap(jvp())/squeeze | solution.py:27
  12.6 350.4 %all-gather.35.cloned.1.call-start = ((), (), s32[]{:S(2)}) async-start(), calls=%async_computation.7 | async-start | bytes 5283840 | tf_op jit(solution)/vmap(jvp())/squeeze | solution.py:27
  13.2 418.5 %all-gather.39.cloned.1.call-start = ((), (), s32[]{:S(2)}) async-start(), calls=%async_computation.9 | async-start | bytes 5283840 | tf_op jit(solution)/vmap(jvp())/squeeze | solution.py:27
  13.8 1178.5 %reduce-scatter.23.cloned.1.call-start = ((), (), s32[]{:S(2)}) async-start(), calls=%async_computation.12 | async-start | bytes 10567680
  402.3 1350.9 %reduce-scatter.25.cloned.1.call-start = ((), (), s32[]{:S(2)}) async-start(), calls=%async_computation.13 | async-start | bytes 10567680
  553.5 1856.0 %reduce-scatter.21.cloned.1.call-start = ((), (), s32[]{:S(2)}) async-start(), calls=%async_computation.11 | async-start | bytes 10567680
  589.5 2476.1 %reduce-scatter.19.cloned.1.call-start = ((), (), s32[]{:S(2)}) async-start(), calls=%async_computation.10 | async-start | bytes 10567680
  1026.6 16.4 collective-permute-start.6
  1027.9 17.0 collective-permute-start.7
  1029.3 32.4 %collective-permute-start.8 = (bf16[24,1024]{1,0:T(8,128)(2,1)S(1)}, bf16[24,1024]{1,0:T(8,128)(2,1)S(1)}, u32[]{:S(2)}, u32[]{:S(2)}) collective-permute-start(bf16[24,1024]{1,0:T(8,128)(2,1)S(1)} %convert.126), channel_id=1, source_target_pairs={{0,9},{1,10},{2,11},{3,12},{4,13},{5,14},{6,15},{7,16},{8,17},{9,1... | collective-permute-start | bytes 147464
  1038.5 27.8 collective-permute-start.9
  1041.4 26.3 collective-permute-start.10
  1043.0 28.4 collective-permute-start.11
  1045.0 28.4 collective-permute-start.12
  1087.5 34.2 %collective-permute-start.24 = (bf16[1024,24]{0,1:T(8,128)(2,1)S(1)}, bf16[1024,24]{0,1:T(8,128)(2,1)S(1)}, u32[]{:S(2)}, u32[]{:S(2)}) collective-permute-start(bf16[1024,24]{0,1:T(8,128)(2,1)S(1)} %convert.127), channel_id=1, source_target_pairs={{0,3},{1,4},{2,5},{3,6},{4,7},{5,8},{6,9},{7,10},{8,11},{9,12},{10... | collective-permute-start | bytes 147464
  1090.5 34.5 %collective-permute-start.25 = (bf16[1024,24]{0,1:T(8,128)(2,1)S(1)}, bf16[1024,24]{0,1:T(8,128)(2,1)S(1)}, u32[]{:S(2)}, u32[]{:S(2)}) collective-permute-start(bf16[1024,24]{0,1:T(8,128)(2,1)S(1)} %convert.127), channel_id=1, source_target_pairs={{0,4},{1,5},{2,6},{3,7},{4,8},{5,9},{6,10},{7,11},{8,12},{9,13},{1... | collective-permute-start | bytes 147464
  1094.3 33.3 %collective-permute-start.26 = (bf16[1024,24]{0,1:T(8,128)(2,1)S(1)}, bf16[1024,24]{0,1:T(8,128)(2,1)S(1)}, u32[]{:S(2)}, u32[]{:S(2)}) collective-permute-start(bf16[1024,24]{0,1:T(8,128)(2,1)S(1)} %convert.127), channel_id=1, source_target_pairs={{0,5},{1,6},{2,7},{3,8},{4,9},{5,10},{6,11},{7,12},{8,13},{9,14},{... | collective-permute-start | bytes 147464
  1096.2 34.2 %collective-permute-start.27 = (bf16[1024,24]{0,1:T(8,128)(2,1)S(1)}, bf16[1024,24]{0,1:T(8,128)(2,1)S(1)}, u32[]{:S(2)}, u32[]{:S(2)}) collective-permute-start(bf16[1024,24]{0,1:T(8,128)(2,1)S(1)} %convert.127), channel_id=1, source_target_pairs={{0,6},{1,7},{2,8},{3,9},{4,10},{5,11},{6,12},{7,13},{8,14},{9,15},... | collective-permute-start | bytes 147464
  1100.0 32.1 %collective-permute-start.28 = (bf16[1024,24]{0,1:T(8,128)(2,1)S(1)}, bf16[1024,24]{0,1:T(8,128)(2,1)S(1)}, u32[]{:S(2)}, u32[]{:S(2)}) collective-permute-start(bf16[1024,24]{0,1:T(8,128)(2,1)S(1)} %convert.127), channel_id=1, source_target_pairs={{0,7},{1,8},{2,9},{3,10},{4,11},{5,12},{6,13},{7,14},{8,15},{9,16}... | collective-permute-start | bytes 147464
  1121.8 30.6 collective-permute-start.29
  1125.0 29.5 collective-permute-start.30
  1127.6 31.1 %collective-permute-start.31 = (bf16[1024,24]{0,1:T(8,128)(2,1)S(1)}, bf16[1024,24]{0,1:T(8,128)(2,1)S(1)}, u32[]{:S(2)}, u32[]{:S(2)}) collective-permute-start(bf16[1024,24]{0,1:T(8,128)(2,1)S(1)} %convert.127), channel_id=1, source_target_pairs={{0,10},{1,11},{2,12},{3,13},{4,14},{5,15},{6,16},{7,17},{8,18},{9,... | collective-permute-start | bytes 147464
  1130.4 29.6 collective-permute-start.32
  1132.1 29.2 collective-permute-start.33
  1162.7 25.1 collective-permute-start.39
  1164.7 23.1 collective-permute-start.40
  1166.1 21.7 collective-permute-start.41
  1169.8 18.0 collective-permute-start.42
  1171.5 16.3 collective-permute-start.22
  (38 other events, 684.6 us)
Sparse Core Ops, SparseCore 0:
  10.9 70.1 all-gather.28
  84.1 65.1 all-gather.30
  153.0 68.5 all-gather.32
  225.2 69.1 all-gather.36
  297.2 65.7 all-gather.34
  366.4 65.1 all-gather.38
  434.0 662.6 reduce-scatter.22
  1099.1 654.0 reduce-scatter.24
  1755.6 653.8 reduce-scatter.20
  2411.8 653.8 reduce-scatter.18
where the time goes:
time: 3080 us; the launch traced here: 3070 us
  waiting for transfers between devices  2140 us (69%)
  blocking collectives  370 us (12%)
  matrix products  316 us (10%)
  starting transfers between devices  117 us (4%)
  other arithmetic  68 us (2%)
  local copies, waits for them, and re-layouts  46.1 us (1%)
    unnamed x58, waiting for transfers between devices  1870 us
    unnamed x1, blocking collectives  370 us
    squeeze x6, waiting for transfers between devices, stack(): h = layer(h, {name: w[number] for name, w in weights.items()})  270 us
    unnamed x48, starting transfers between devices  117 us
    dot_general x6, matrix products, layer(): up = jnp.dot(a, w['w_up'], preferred_element_type=jnp.float32)  115 us
    dot_general x6, matrix products, layer(): gate = jnp.dot(a, w['w_gate'], preferred_element_type=jnp.float32)  103 us
    dot_general x5, matrix products, matmul(): jnp.dot(a, w, preferred_element_type=jnp.float32).astype(jnp.bfloat16)  98.2 us
  transfers between devices with their start and end apart: 54, of which 9 were waited for; matrix products, arithmetic and copies ran while one was open for 25% of the time, Pallas kernels for 0%

commit v1 on v0

v1 whole, which is shorter than its diff:
```python
import functools
import jax, jax.numpy as jnp
from jax import lax
from jax.experimental import pallas as pl
from jax.experimental.pallas import tpu as pltpu
from jax.sharding import PartitionSpec as P
T, D, FF, NT, FT = 2048, 1024, 2560, 5, 512
MB = 512
LANES = 128
f32, bf16 = jnp.float32, jnp.bfloat16
def dot(a, b): return jnp.dot(a, b, preferred_element_type=f32)
def dot_t(a, b): return lax.dot_general(a, b, (((1,), (1,)), ((), ())), preferred_element_type=f32)

def norm_into(h_ref, a_ref, rows=256):
    @pl.loop(0, T // rows)
    def _(i):
        r = pl.ds(pl.multiple_of(i * rows, rows), rows)
        w = h_ref[r, :].astype(f32)
        s = lax.rsqrt(jnp.mean(w * w, -1, keepdims=True) + 1e-6)
        a_ref[r, :] = (w * s).astype(bf16)

def fwd0_kernel(base, x_ref, wg_hbm, wu_hbm, wd_hbm, h1_ref, g_hbm, u_hbm, at_hbm,
                a, act, wg, wu, wd, gbuf, ubuf, atbuf, wsem, dsem, osem):
    def wcopy(t, s):
        return (pltpu.make_async_copy(wg_hbm.at[base * NT + t], wg.at[s], wsem.at[0, s]),
                pltpu.make_async_copy(wu_hbm.at[base * NT + t], wu.at[s], wsem.at[1, s]))
    dcopies = [pltpu.make_async_copy(wd_hbm.at[base * 4 + j // 2, j % 2], wd.at[:, pl.ds(LANES * j, LANES)], dsem.at[j]) for j in range(8)]
    for c in wcopy(0, 0): c.start()
    for c in dcopies: c.start()
    norm_into(x_ref, a)
    def ocopy(t, m, s):
        r = pl.ds(pl.multiple_of(m * MB, MB), MB)
        return (pltpu.make_async_copy(gbuf.at[s], g_hbm.at[t, r], osem.at[0, s]),
                pltpu.make_async_copy(ubuf.at[s], u_hbm.at[t, r], osem.at[1, s]),
                pltpu.make_async_copy(atbuf.at[s], at_hbm.at[t, :, r], osem.at[2, s]))
    NM = T // MB
    @pl.loop(0, NT * NM)
    def _(i):
        t = i // NM; m = i % NM; s = t % 2; o = i % 2
        @pl.when(m == 0)
        def _():
            for c in wcopy(t, s): c.wait()
            @pl.when(t + 1 < NT)
            def _():
                for c in wcopy(t + 1, 1 - s): c.start()
        @pl.when(i >= 2)
        def _():
            for c in ocopy(t, m, o): c.wait()
        r = pl.ds(pl.multiple_of(m * MB, MB), MB)
        am = a[r, :]
        g = dot(am, wg[s]); u = dot(am, wu[s])
        gbuf[o] = g; ubuf[o] = u
        ac = (g * jax.nn.sigmoid(g) * u).astype(bf16)
        act[t, r, :] = ac
        atbuf[o] = ac.T
        for c in ocopy(t, m, o): c.start()
    for c in dcopies: c.wait()
    @pl.loop(0, NM)
    def _(m):
        r = pl.ds(pl.multiple_of(m * MB, MB), MB)
        acc = dot(act[0, r, :], wd[0:FT, :])
        for t in range(1, NT):
            acc += dot(act[t, r, :], wd[t * FT:(t + 1) * FT, :])
        h1_ref[r, :] = (x_ref[r, :].astype(f32) + acc.astype(bf16).astype(f32)).astype(bf16)
    for i in (NT * NM - 2, NT * NM - 1):
        for c in ocopy(i // NM, i % NM, i % 2): c.wait()

ANY = pl.BlockSpec(memory_space=pl.ANY)
VM = pl.BlockSpec(memory_space=pltpu.VMEM)
def fwd0(x, wg, wu, wd):
    return pl.pallas_call(
        functools.partial(fwd0_kernel, 0), name="fwd0",
        out_shape=[jax.ShapeDtypeStruct((T, D), bf16), jax.ShapeDtypeStruct((NT, T, FT), f32), jax.ShapeDtypeStruct((NT, T, FT), f32), jax.ShapeDtypeStruct((NT, FT, T), bf16)],
        in_specs=[VM, ANY, ANY, ANY], out_specs=[VM, ANY, ANY, ANY],
        scratch_shapes=[pltpu.VMEM((T, D), bf16), pltpu.VMEM((NT, T, FT), bf16), pltpu.VMEM((2, D, FT), bf16), pltpu.VMEM((2, D, FT), bf16), pltpu.VMEM((FF, D), bf16),
                        pltpu.VMEM((2, MB, FT), f32), pltpu.VMEM((2, MB, FT), f32), pltpu.VMEM((2, FT, MB), bf16),
                        pltpu.SemaphoreType.DMA((2, 2)), pltpu.SemaphoreType.DMA((8,)), pltpu.SemaphoreType.DMA((3, 2))],
        compiler_params=pltpu.CompilerParams(vmem_limit_bytes=60 << 20),
    )(x, wg, wu, wd)

def dact_part(g, u, da):
    s = jax.nn.sigmoid(g)
    p = g * s
    return (da * u * (s + p * (1 - s))).astype(bf16), (da * p).astype(bf16), p

def norm_back(h, da, dh):
    w = h.astype(f32)
    s = lax.rsqrt(jnp.mean(w * w, -1, keepdims=True) + 1e-6)
    d = da.astype(bf16).astype(f32)
    c = jnp.sum(d * w, -1, keepdims=True) * (s * s * s / D)
    return (dh.astype(f32) + (d * s - w * c).astype(bf16).astype(f32)).astype(bf16)

def bwd_kernel(first, *refs):
    base = int(first)
    if first:
        (h_ref, dh_ref, wg_hbm, wu_hbm, wd_hbm, dx_ref, dwg_hbm, dwu_hbm, dwd_hbm,
         a, at, acc, dg, du, wg, wu, wd, ob, actt, dob, wsem, osem, asem, dsem) = refs
    else:
        (h_ref, dh_ref, g_hbm, u_hbm, at_hbm, wg_hbm, wu_hbm, wd_hbm, dx_ref, dwg_hbm, dwu_hbm, dwd_hbm,
         a, at, acc, dg, du, wg, wu, wd, ob, actt, dob, gb, ub, wsem, osem, asem, dsem, gsem) = refs
    NM = T // MB
    def wcopy(t, s):
        tt = pl.ds(t * FT, FT) if isinstance(t, int) else pl.ds(pl.multiple_of(t * FT, FT), FT)
        return [pltpu.make_async_copy(wg_hbm.at[base * NT + t], wg.at[s], wsem.at[0, s]),
                pltpu.make_async_copy(wu_hbm.at[base * NT + t], wu.at[s], wsem.at[1, s])] + [
                pltpu.make_async_copy(wd_hbm.at[base * 4 + j // 2, j % 2, tt], wd.at[s, :, pl.ds(LANES * j, LANES)], wsem.at[2 + j, s]) for j in range(8)]
    def gcopy(i, s):
        t = i // NM; m = i % NM
        r = pl.ds(m * MB if isinstance(m, int) else pl.multiple_of(m * MB, MB), MB)
        return [pltpu.make_async_copy(g_hbm.at[t, r], gb.at[s], gsem.at[0, s]), pltpu.make_async_copy(u_hbm.at[t, r], ub.at[s], gsem.at[1, s])]
    def ocopy(t, s):
        return [pltpu.make_async_copy(ob.at[s, 0], dwg_hbm.at[t], osem.at[0, s]), pltpu.make_async_copy(ob.at[s, 1], dwu_hbm.at[t], osem.at[1, s])]
    for c in wcopy(0, 0): c.start()
    if not first:
        for c in gcopy(0, 0): c.start()
        for t in range(NT): pltpu.make_async_copy(at_hbm.at[t], actt.at[t], asem.at[t]).start()
    rows = 256
    @pl.loop(0, T // rows)
    def _(i):
        r = pl.ds(pl.multiple_of(i * rows, rows), rows)
        w = h_ref[r, :].astype(f32)
        s = lax.rsqrt(jnp.mean(w * w, -1, keepdims=True) + 1e-6)
        av = (w * s).astype(bf16)
        if first: a[r, :] = av
        at[:, r] = av.T
    @pl.loop(0, NT)
    def _(t):
        s = t % 2
        for c in wcopy(t, s): c.wait()
        @pl.when(t + 1 < NT)
        def _():
            for c in wcopy(t + 1, 1 - s): c.start()
        @pl.loop(0, NM)
        def _(m):
            r = pl.ds(pl.multiple_of(m * MB, MB), MB)
            i = t * NM + m
            if first:
                am = a[r, :]
                g = dot(am, wg[s]); u = dot(am, wu[s])
            else:
                o = i % 2
                for c in gcopy(i, o): c.wait()
                @pl.when(i + 1 < NT * NM)
                def _():
                    for c in gcopy(i + 1, 1 - o): c.start()
                g = gb[o]; u = ub[o]
            da = dot_t(dh_ref[r, :], wd[s]).astype(bf16).astype(f32)
            dgv, duv, p = dact_part(g, u, da)
            dg[r, :] = dgv; du[r, :] = duv
            if first: actt[t, :, r] = (p * u).astype(bf16).T
            v = dot_t(dgv, wg[s]) + dot_t(duv, wu[s])
            @pl.when(t == 0)
            def _(): acc[r, :] = v
            @pl.when(t > 0)
            def _(): acc[r, :] += v
        @pl.when(t >= 2)
        def _():
            for c in ocopy(t, s): c.wait()
        @pl.loop(0, D // 512)
        def _(k):
            r = pl.ds(pl.multiple_of(k * 512, 512), 512)
            ob[s, 0, r, :] = dot(at[r, :], dg[...]).astype(bf16)
            ob[s, 1, r, :] = dot(at[r, :], du[...]).astype(bf16)
        for c in ocopy(t, s): c.start()
    @pl.loop(0, NM)
    def _(m):
        r = pl.ds(pl.multiple_of(m * MB, MB), MB)
        dx_ref[r, :] = norm_back(h_ref[r, :], acc[r, :], dh_ref[r, :])
    if not first:
        for t in range(NT): pltpu.make_async_copy(at_hbm.at[t], actt.at[t], asem.at[t]).wait()
    def dcopy(q, s):
        return [pltpu.make_async_copy(dob.at[s, j], dwd_hbm.at[q, j], dsem.at[j, s]) for j in range(2)]
    for q in range(4):
        s = q % 2
        if q >= 2:
            for c in dcopy(q - 2, s): c.wait()
        @pl.loop(0, NT)
        def _(t):
            v = dot(actt[t], dh_ref[:, 256 * q:256 * q + 256]).astype(bf16)
            r = pl.ds(pl.multiple_of(t * FT, FT), FT)
            dob[s, 0, r, :] = v[:, :LANES]
            dob[s, 1, r, :] = v[:, LANES:]
        for c in dcopy(q, s): c.start()
    for q in (2, 3):
        for c in dcopy(q, q % 2): c.wait()
    for t in (NT - 2, NT - 1):
        for c in ocopy(t, t % 2): c.wait()

def bwd(first, h, dh, *rest):
    n = len(rest)
    scr = [pltpu.VMEM((T, D) if first else (16, LANES), bf16), pltpu.VMEM((D, T), bf16), pltpu.VMEM((T, D), f32), pltpu.VMEM((T, FT), bf16), pltpu.VMEM((T, FT), bf16),
           pltpu.VMEM((2, D, FT), bf16), pltpu.VMEM((2, D, FT), bf16), pltpu.VMEM((2, FT, D), bf16), pltpu.VMEM((2, 2, D, FT), bf16),
           pltpu.VMEM((NT, FT, T), bf16), pltpu.VMEM((2, 2, FF, LANES), bf16)]
    if not first: scr += [pltpu.VMEM((2, MB, FT), f32)] * 2
    scr += [pltpu.SemaphoreType.DMA((10, 2)), pltpu.SemaphoreType.DMA((2, 2)), pltpu.SemaphoreType.DMA((NT,)), pltpu.SemaphoreType.DMA((2, 2))]
    if not first: scr += [pltpu.SemaphoreType.DMA((2, 2))]
    return pl.pallas_call(
        functools.partial(bwd_kernel, first), name="bwd1" if first else "bwd0",
        out_shape=[jax.ShapeDtypeStruct((T, D), bf16), jax.ShapeDtypeStruct((NT, D, FT), bf16), jax.ShapeDtypeStruct((NT, D, FT), bf16), jax.ShapeDtypeStruct((4, 2, FF, LANES), bf16)],
        in_specs=[VM, VM] + [ANY] * n, out_specs=[VM, ANY, ANY, ANY],
        scratch_shapes=scr, compiler_params=pltpu.CompilerParams(vmem_limit_bytes=64 * 2**20 - 2**16),
    )(h, dh, *rest)


def compute(x, dy, wg, wu, wd):
    h1, g0, u0, at0 = fwd0(x, wg, wu, wd)
    dh1, *dw1 = bwd(True, h1, dy, wg, wu, wd)
    dx, *dw0 = bwd(False, x, dh1, g0, u0, at0, wg, wu, wd)
    return dx, dw0, dw1

STRIDE = {"x": 32, "y": 8, "z": 2}
AXES = ("x", "y", "z")
ORDER = (("x", "y", "z"), ("y", "z", "x"), ("z", "x", "y"))
LEFT, RIGHT = 3, 1

class Place:
    def __init__(self):
        me = lax.axis_index("dp")
        self.me = me
        self.core = me % 2
        self.at = {"x": me // 32, "y": me // 8 % 4, "z": me // 2 % 4}
    def ring(self, axis, d):
        return (self.at[axis] + d) % 4
    def near(self, axis, d):
        return {"dp": self.me + (self.ring(axis, d) - self.at[axis]) * STRIDE[axis]}
    def partner(self):
        return {"dp": self.me + 1 - 2 * self.core}
    def all(self):
        return [self.partner()] + [self.near(a, d) for a in AXES for d in (LEFT, RIGHT)]

def enter(place):
    barrier = pltpu.get_barrier_semaphore()
    for other in place.all():
        pl.semaphore_signal(barrier, inc=1, device_id=other)
    pl.semaphore_wait(barrier, 7)

def remote(src, dst, send, recv, to):
    return pltpu.make_async_remote_copy(src_ref=src, dst_ref=dst, send_sem=send, recv_sem=recv, device_id=to)

def mult(x, n):
    return x if isinstance(x, int) else pl.multiple_of(x, n)

class Gather:
    STAGES = 8
    def __init__(self, place, ins, outs, send, recv, local):
        self.p, self.ins, self.outs, self.send, self.recv, self.local = place, ins, outs, send, recv, local
    def own(self, c, q):
        if c < 2:
            return self.ins[c].at[q // 5, :, pl.ds(mult(q % 5 * 512, 512), 512)]
        return self.ins[2].at[q // 4, :, pl.ds(mult(q % 4 * 256 + self.p.core * LANES, LANES), LANES)]
    def part(self, c, q, phase, r, half=None, own=False):
        o = ORDER[c]
        pos = {a: slice(None) if j < phase else (r if j == phase else self.p.at[a]) for j, a in enumerate(o)}
        rows = cols = slice(None)
        if half is not None:
            if phase > 0:
                pos[o[0]] = pl.ds(2 * half, 2)
            elif c < 2:
                cols = pl.ds(256 * half, 256)
            else:
                rows = pl.ds(24 * half, 16 if half else 24)
        i = tuple(pos[a] for a in AXES)
        out = self.outs[c]
        return out.at[(q, *i, self.p.core, rows, cols)] if c < 2 else out.at[(q, self.p.core, *i, rows, cols)]
    def sem(self, q, c, k):
        return self.send.at[q, c, k], self.recv.at[q, c, k]
    def copies(self, s, c, q):
        p = self.p
        if s == 6:
            half = self.outs[c].at[q, :, :, :, p.core] if c < 2 else self.outs[c].at[q, p.core]
            return [remote(half, half, *self.sem(q, c, 12), p.partner())]
        phase = s // 2
        a = ORDER[c][phase]
        here = p.at[a]
        k = 4 * phase + 2 * (s % 2)
        if s % 2 == 0:
            dst = self.part(c, q, phase, here)
            src = self.own(c, q) if s == 0 else dst
            return [remote(src, dst, *self.sem(q, c, k), p.near(a, RIGHT)), remote(src, dst, *self.sem(q, c, k + 1), p.near(a, LEFT))]
        l, r = self.part(c, q, phase, p.ring(a, LEFT), 0), self.part(c, q, phase, p.ring(a, RIGHT), 1)
        return [remote(l, l, *self.sem(q, c, k), p.near(a, RIGHT)), remote(r, r, *self.sem(q, c, k + 1), p.near(a, LEFT))]
    def keep(self, c, q):
        return pltpu.make_async_copy(self.own(c, q), self.part(c, q, 0, self.p.at[ORDER[c][0]]), self.local.at[q, c])
    def stage(self, s, c, q):
        if s > 0:
            for x in self.copies(s - 1, c, q): x.wait()
        if s == 0:
            self.keep(c, q).start()
        if s == 2:
            self.keep(c, q).wait()
        if s < 7:
            for x in self.copies(s, c, q): x.start()

def join_down(place, w_in, peer, chip, sem):
    x = remote(w_in, peer, sem.at[0], sem.at[1], place.partner())
    x.start(); x.wait()
    first = place.core == 0
    mine, other = w_in[...].astype(f32), peer[...].astype(f32)
    top, bottom = jnp.where(first, mine, other), jnp.where(first, other, mine)
    chip[...] = jnp.concatenate([top, bottom], axis=1).astype(bf16)

def gather_kernel(wg, wu, wd, og, ou, od, peer, chip, send, recv, local, jsem):
    place = Place()
    enter(place)
    join_down(place, wd, peer, chip, jsem)
    g = Gather(place, (wg, wu, chip), (og, ou, od), send, recv, local)
    @pl.loop(0, 2 * 9 + 8)
    def _(i):
        for s in reversed(range(8)):
            q = (i - s) // 2
            ok = (i >= s) & ((i - s) % 2 == 0) & (q < 10)
            @pl.when(ok)
            def _():
                for c in (0, 1): g.stage(s, c, q)
            @pl.when(ok & (q % 5 < 4))
            def _():
                g.stage(s, 2, q // 5 * 4 + q % 5)

VM = pl.BlockSpec(memory_space=pltpu.VMEM)
ANY = pl.BlockSpec(memory_space=pl.ANY)
def gather(wg, wu, wd):
    return pl.pallas_call(
        gather_kernel, name="gather",
        out_shape=[jax.ShapeDtypeStruct((10, 4, 4, 4, 2, 8, 512), bf16)] * 2 + [jax.ShapeDtypeStruct((8, 2, 4, 4, 4, 40, LANES), bf16)],
        in_specs=[VM] * 3, out_specs=[ANY] * 3,
        scratch_shapes=[pltpu.VMEM((2, 20, 1024), bf16), pltpu.VMEM((2, 40, 1024), bf16),
                        pltpu.SemaphoreType.DMA((10, 3, 13)), pltpu.SemaphoreType.DMA((10, 3, 13)), pltpu.SemaphoreType.DMA((10, 3)), pltpu.SemaphoreType.DMA((2,))],
        compiler_params=pltpu.CompilerParams(collective_id=0, has_side_effects=True, vmem_limit_bytes=60 << 20),
    )(wg, wu, wd)

def parts_shape(c, phase):
    o = ORDER[c]
    n = {a: 4 if j < phase else (2 if j == phase else 1) for j, a in enumerate(o)}
    return tuple(n[a] for a in AXES) + ((8, 512) if c < 2 else (40, LANES))

class Scatter:
    STAGES = 9
    def __init__(self, place, tile, sums, halves, wholes, outs, fin, send, recv, credit, osem):
        self.p, self.tile, self.sums, self.halves, self.wholes, self.outs, self.fin = place, tile, sums, halves, wholes, outs, fin
        self.send, self.recv, self.credit, self.osem = send, recv, credit, osem
    def where(self, c, phase, r, half, ring):
        o = ORDER[c]
        pos = {a: slice(None) if j < phase else (r if j == phase else (self.p.at[a] if ring is None else 0)) for j, a in enumerate(o)}
        rows = cols = slice(None)
        if half is not None:
            if phase > 0:
                pos[o[0]] = pl.ds(2 * half, 2)
            elif c < 2:
                cols = pl.ds(256 * half, 256)
            else:
                rows = pl.ds(24 * half, 16 if half else 24)
        return (*(pos[a] for a in AXES), rows, cols)
    def part(self, c, slot, phase, r, half=None):
        return self.sums[c], (slot, *self.where(c, phase, r, half, None))
    def half_of(self, c, slot, phase, d):
        return self.halves[c][phase], (slot, *self.where(c, phase, d, d, 0))
    def whole_of(self, c, slot, phase, d):
        return self.wholes[c][phase], (slot, *self.where(c, phase, d, None, 0))
    def sem(self, slot, c, k):
        return self.send.at[slot, c, k], self.recv.at[slot, c, k]
    def copies(self, s, c, q, slot):
        p = self.p
        at = lambda x: x[0].at[x[1]]
        if s == 0:
            t = self.tile(c, slot)
            src = t.at[:, :, :, 1 - p.core] if c < 2 else t.at[1 - p.core]
            return [remote(src, self.sums[c].at[slot], *self.sem(slot, c, 12), p.partner())]
        if s == 7:
            fin = at(self.part(c, slot, 0, p.at[ORDER[c][0]]))
            if c < 2:
                return [pltpu.make_async_copy(fin, self.outs[c].at[q // 5, :, pl.ds(mult(q % 5 * 512, 512), 512)], self.osem.at[slot, c])]
            return [remote(fin, self.fin.at[q // 4, :, pl.ds(mult(q % 4 * 256 + p.core * LANES, LANES), LANES)], *self.sem(slot, c, 13), p.partner())]
        phase = 2 - (s - 1) // 2
        a = ORDER[c][phase]
        k = 4 * phase + 2 * ((s - 1) % 2)
        if s % 2 == 1:
            two = [(at(self.part(c, slot, phase, p.ring(a, 2), d)), at(self.half_of(c, slot, phase, d))) for d in (0, 1)]
        else:
            two = [(at(self.part(c, slot, phase, p.ring(a, (RIGHT, LEFT)[d]))), at(self.whole_of(c, slot, phase, d))) for d in (0, 1)]
        return [remote(*two[d], *self.sem(slot, c, k + d), p.near(a, (RIGHT, LEFT)[d])) for d in (0, 1)]
    def add(self, into, *terms):
        ref, i = into
        v = ref[i].astype(f32)
        for r, j in terms: v = v + r[j].astype(f32)
        ref[i] = v.astype(bf16)
    def stage(self, s, c, q, slot, wait_credit=None):
        p = self.p
        if s > 0:
            for x in self.copies(s - 1, c, q, slot): x.wait()
        if s == 0:
            @pl.when(wait_credit)
            def _():
                for i in range(7): pl.semaphore_wait(self.credit.at[c, i], 1)
        elif s == 1:
            t = self.tile(c, slot)
            @pl.loop(0, 4)
            def _(x):
                mine = t[x, :, :, p.core] if c < 2 else t[p.core, x]
                self.sums[c][slot, x] = (mine.astype(f32) + self.sums[c][slot, x].astype(f32)).astype(bf16)
        elif s == 8:
            if c == 2:
                i = (q // 4, slice(None), pl.ds(mult(q % 4 * 256 + p.core * LANES, LANES), LANES))
                ref, j = self.part(c, slot, 0, p.at[ORDER[c][0]])
                self.fin[i] = ref[j]
        else:
            phase = 2 - (s - 2) // 2
            a = ORDER[c][phase]
            if s % 2 == 0:
                for d in (0, 1):
                    self.add(self.part(c, slot, phase, p.ring(a, (RIGHT, LEFT)[d]), d), self.half_of(c, slot, phase, d))
            else:
                self.add(self.part(c, slot, phase, p.at[a]), *(self.whole_of(c, slot, phase, d) for d in (0, 1)))
        if s < 8:
            for x in self.copies(s, c, q, slot): x.start()
    def release(self, c):
        for i, other in enumerate(self.p.all()):
            pl.semaphore_signal(self.credit.at[c, (0, 2, 1, 4, 3, 6, 5)[i]], inc=1, device_id=other)
    def finish_down(self, out):
        first = self.p.core == 0
        v = self.fin[...].astype(f32)
        out[...] = jnp.where(first, v[:, :20], v[:, 20:]).astype(bf16)

def scatter_scratch(slots=2):
    sums = [pltpu.VMEM((slots, 4, 4, 4, 8, 512), bf16)] * 2 + [pltpu.VMEM((slots, 4, 4, 4, 40, LANES), bf16)]
    rings = [pltpu.VMEM((slots, *parts_shape(c, ph)), bf16) for c in range(3) for ph in range(3)]
    return sums + rings * 2 + [pltpu.VMEM((2, 40, 1024), bf16), pltpu.SemaphoreType.DMA((slots, 3, 14)), pltpu.SemaphoreType.DMA((slots, 3, 14)),
                               pltpu.SemaphoreType.REGULAR((3, 7)), pltpu.SemaphoreType.DMA((slots, 2))]

def make_scatter(place, tile, outs, refs):
    sums, halves, wholes = refs[:3], refs[3:12], refs[12:21]
    fin, send, recv, credit, osem = refs[21:26]
    nine = lambda r: [r[3 * c:3 * c + 3] for c in range(3)]
    return Scatter(place, tile, sums, nine(halves), nine(wholes), outs, fin, send, recv, credit, osem)

def scatter_kernel(g0, u0, d0, g1, u1, d1, og, ou, od, tg, tu, td, tsem, *refs):
    place = Place()
    enter(place)
    tiles, hbm = (tg, tu, td), ((g0, u0, d0), (g1, u1, d1))
    sc = make_scatter(place, lambda c, slot: tiles[c].at[slot], (og, ou), refs)
    def load(c, q, slot):
        n = 5 if c < 2 else 4
        for l in (0, 1):
            @pl.when(q // n == l)
            def _():
                x = pltpu.make_async_copy(hbm[l][c].at[q % n], tiles[c].at[slot], tsem.at[slot, c])
                x.start(); x.wait()
    EVERY = 5
    @pl.loop(0, EVERY * 9 + 9)
    def _(i):
        for s in reversed(range(9)):
            q = (i - s) // EVERY
            slot = q % 2
            ok = (i >= s) & ((i - s) % EVERY == 0) & (q < 10)
            def go(c, n, q):
                if s == 0:
                    load(c, q, slot)
                sc.stage(s, c, q, slot, q_all >= 2 if s == 0 else None)
                if s == 8:
                    @pl.when(q_all < n - 2)
                    def _(): sc.release(c)
            q_all = q
            @pl.when(ok)
            def _():
                for c in (0, 1): go(c, 10, q)
            @pl.when(ok & (q < 8))
            def _(): go(2, 8, q)
    sc.finish_down(od)

def scatter(*terms):
    return pl.pallas_call(
        scatter_kernel, name="scatter",
        out_shape=[jax.ShapeDtypeStruct((2, 8, 2560), bf16)] * 2 + [jax.ShapeDtypeStruct((2, 20, 1024), bf16)],
        in_specs=[ANY] * 6, out_specs=[ANY, ANY, VM],
        scratch_shapes=[pltpu.VMEM((2, 4, 4, 4, 2, 8, 512), bf16)] * 2 + [pltpu.VMEM((2, 2, 4, 4, 4, 40, LANES), bf16), pltpu.SemaphoreType.DMA((2, 3))] + scatter_scratch(),
        compiler_params=pltpu.CompilerParams(collective_id=1, has_side_effects=True, vmem_limit_bytes=60 << 20),
    )(*terms)


def solution(mesh):
    def step(x, dy, wg, wu, wd):
        tg, tu, td = gather(wg, wu, wd)
        tg, tu, td = tg.reshape(2 * NT, D, FT), tu.reshape(2 * NT, D, FT), td.reshape(8, 2, FF, LANES)
        dx, dw0, dw1 = compute(x[0], dy[0], tg, tu, td)
        shape = ((NT, 4, 4, 4, 2, 8, 512), (NT, 4, 4, 4, 2, 8, 512), (4, 2, 4, 4, 4, 40, LANES))
        terms = [v.reshape(s) for dw in (dw0, dw1) for v, s in zip(dw, shape)]
        return (dx[None], *scatter(*terms))

    tokens, rows = P(("rep", "dp")), P(None, "dp", None)
    return jax.shard_map(step, mesh=mesh, in_specs=(tokens, tokens, rows, rows, rows), out_specs=(tokens,) + (P("rep", "dp", None),) * 3, check_vma=False)
```

time: 3080 us -> 649 us (0.21)
  waiting for transfers between devices: 2140 us -> 0 us
  Pallas kernels: 0 us -> 640 us
  blocking collectives: 370 us -> 0 us
  matrix products: 316 us -> 0 us
  starting transfers between devices: 117 us -> 0 us
  other arithmetic: 68 us -> 0 us
  local copies, waits for them, and re-layouts: 46.1 us -> 6.21 us
    unnamed x58 -> x0, waiting for transfers between devices: 1870 us -> none
    pallas_call x0 -> x5, Pallas kernels: none -> 640 us  [the longest x1 239 us: scatter(): pl.pallas_call(scatter_kernel, name='scatter', out_shape=[jax.ShapeDtypeS...]
    unnamed x1 -> x0, blocking collectives: 370 us -> none
    dot_general x17 -> x0, matrix products: 316 us -> none  [the longest x6 115 us: layer(): up = jnp.dot(a, w['w_up'], preferred_element_type=jnp.float32)]
    squeeze x6 -> x0, waiting for transfers between devices: 270 us -> none  [stack(): h = layer(h, {name: w[number] for name, w in weights.items()})]
    unnamed x48 -> x0, starting transfers between devices: 117 us -> none
    unnamed x5 -> x0, other arithmetic: 52 us -> none
    unnamed x40 -> x4, local copies, waits for them, and re-layouts: 41.4 us -> 6.21 us
  transfers between devices with their start and end apart: 54 -> 0, of which waited for: 9 -> 0; matrix products, arithmetic and copies ran while one was open for 25% -> 0% of each run, Pallas kernels for 0% -> 0%
where the time goes in v1:
time: 649 us; the launch traced here: 647 us
  Pallas kernels  640 us (99%)
    pallas_call x1, Pallas kernels, scatter(): pl.pallas_call(scatter_kernel, name='scatter', out_shape=[jax.ShapeDtypeS...  239 us
    pallas_call x2, Pallas kernels, bwd(): pl.pallas_call(functools.partial(bwd_kernel, first), name='bwd1' if first...  219 us
    pallas_call x1, Pallas kernels, gather(): pl.pallas_call(gather_kernel, name='gather', out_shape=[jax.ShapeDtypeStr...  135 us
    pallas_call x1, Pallas kernels, fwd0(): pl.pallas_call(functools.partial(fwd0_kernel, 0), name='fwd0', out_shape=...  46.3 us

profile of v1, /device:TPU:0, one launch (start us, length us, event | category | flops | bytes accessed | tf_op | source)
XLA Modules:
  0.0 646.8 jit_solution(5186977774077798418)
XLA Ops:
  0.6 1.5 copy.9.wd
  2.2 135.1 %gather.1 = (bf16[10,4,4,4,2,8,512]{6,5,4,3,2,1,0:T(8,128)(2,1)}, bf16[10,4,4,4,2,8,512]{6,5,4,3,2,1,0:T(8,128)(2,1)}, bf16[8,2,4,4,4,40,128]{6,5,4,3,2,1,0:T(8,128)(2,1)}) custom-call(bf16[2,8,2560]{2,1,0:T(8,128)(2,1)} %wg.1, bf16[2,8,2560]{2,1,0:T(8,128)(2,1)} %wu.1, bf16[2,20,1024]{2,1,0:T(8,128)(2,1)} %copy.9.wd), custom_call_target="tpu_custom_call" | custom-call | tf_op jit(solution)/shard_map/gather/pallas_call | solution.py:322
  137.3 46.3 %fwd0.1 = (bf16[2048,1024]{1,0:T(8,128)(2,1)}, f32[5,2048,512]{2,1,0:T(8,128)}, f32[5,2048,512]{2,1,0:T(8,128)}, bf16[5,512,2048]{2,1,0:T(8,128)(2,1)}) custom-call(bf16[2048,1024]{1,0:T(8,128)(2,1)} %bitcast.21, bf16[10,1024,512]{2,1,0:T(8,128)(2,1)} %bitcast.12, bf16[10,1024,512]{2,1,0:T(8,128)(2,1)} %bitcast.15, bf16[8,2,2560,128]{3,2,1,0:T(8,128)(2,1)} %bitcast.18), custom_call_target="tpu_custom_call" | custom-call | tf_op jit(solution)/shard_map/fwd0/pallas_call | solution.py:71
  183.6 117.6 %bwd1.1 = (bf16[2048,1024]{1,0:T(8,128)(2,1)}, bf16[5,1024,512]{2,1,0:T(8,128)(2,1)}, bf16[5,1024,512]{2,1,0:T(8,128)(2,1)}, bf16[4,2,2560,128]{3,2,1,0:T(8,128)(2,1)}) custom-call(bf16[2048,1024]{1,0:T(8,128)(2,1)} %get-tuple-element.25.refs_0_, bf16[2048,1024]{1,0:T(8,128)(2,1)} %bitcast.29, bf16[10,1024,512]{2,1,0:T(8,128)(2,1)} %bitcast.13, ...), custom_call_target="tpu_custom_call" | custom-call | tf_op jit(solution)/shard_map/bwd1/pallas_call | solution.py:197
  301.2 101.7 %bwd0.1 = (bf16[2048,1024]{1,0:T(8,128)(2,1)}, bf16[5,1024,512]{2,1,0:T(8,128)(2,1)}, bf16[5,1024,512]{2,1,0:T(8,128)(2,1)}, bf16[4,2,2560,128]{3,2,1,0:T(8,128)(2,1)}) custom-call(bf16[2048,1024]{1,0:T(8,128)(2,1)} %bitcast.22, bf16[2048,1024]{1,0:T(8,128)(2,1)} %get-tuple-element.26.refs_1_, f32[5,2048,512]{2,1,0:T(8,128)} %get-tuple-element.27.refs_2_, ...), custom_call_target="tpu_custom_call" | custom-call | tf_op jit(solution)/shard_map/bwd0/pallas_call | solution.py:197
  402.8 239.3 %scatter.1 = (bf16[2,8,2560]{2,1,0:T(8,128)(2,1)}, bf16[2,8,2560]{2,1,0:T(8,128)(2,1)}, bf16[2,20,1024]{2,1,0:T(8,128)(2,1)}) custom-call(bf16[5,4,4,4,2,8,512]{6,5,4,3,2,1,0:T(8,128)(2,1)} %bitcast.26, bf16[5,4,4,4,2,8,512]{6,5,4,3,2,1,0:T(8,128)(2,1)} %bitcast.27, bf16[4,2,4,4,4,40,128]{6,5,4,3,2,1,0:T(8,128)(2,1)} %bitcast.28, ...), custom_call_target="tpu_custom_call" | custom-call | tf_op jit(solution)/shard_map/scatter/pallas_call | solution.py:470
  642.2 1.6 copy.10
  643.8 1.5 copy.13
  645.3 1.5 copy.14

commit v2 on v0

v2 whole, which is shorter than its diff:
```python
import functools
import jax, jax.numpy as jnp
from jax import lax
from jax.experimental import pallas as pl
from jax.experimental.pallas import tpu as pltpu
from jax.sharding import PartitionSpec as P

f32, bf16 = jnp.float32, jnp.bfloat16
T, D, FF = 2048, 1024, 2560
NT, FT = 5, 512
NQ, LANES = 4, 128
MB = 512
NM = T // MB
ROWS = FF // 4
AXES = ("x", "y", "z")
STRIDE = {"x": 32, "y": 8, "z": 2}
ORDER = (("x", "y", "z"), ("y", "z", "x"), ("z", "x", "y"))
LEFT, RIGHT, ACROSS = 3, 1, 2
GU, DOWN = (0, 1), 2
CHIPS = (4, 4, 4)
BLOCK = ((8, FT), (8, FT), (40, LANES))
TILE = ((*CHIPS, 2, *BLOCK[0]), (*CHIPS, 2, *BLOCK[1]), (2, *CHIPS, *BLOCK[DOWN]))
NTILES = (NT, NT, NQ)
ALL = slice(None)


def dot(a, b):
    return jnp.dot(a, b, preferred_element_type=f32)


def dot_t(a, b):
    return lax.dot_general(a, b, (((1,), (1,)), ((), ())), preferred_element_type=f32)


def mult(x, n):
    return x if isinstance(x, int) else pl.multiple_of(x, n)


def span(i, n):
    return pl.ds(mult(i * n, n), n)


def normed(h):
    w = h.astype(f32)
    return (w * lax.rsqrt(jnp.mean(w * w, -1, keepdims=True) + 1e-6)).astype(bf16)


def norm_back(h, da, dh):
    w = h.astype(f32)
    s = lax.rsqrt(jnp.mean(w * w, -1, keepdims=True) + 1e-6)
    d = da.astype(bf16).astype(f32)
    c = jnp.sum(d * w, -1, keepdims=True) * (s * s * s / D)
    return (dh.astype(f32) + (d * s - w * c).astype(bf16).astype(f32)).astype(bf16)


class Place:
    def __init__(self):
        self.me = lax.axis_index("dp")
        self.core = self.me % 2
        self.at = {a: self.me // STRIDE[a] % 4 for a in AXES}

    def ring(self, axis, d):
        return (self.at[axis] + d) % 4

    def near(self, axis, d):
        return {"dp": self.me + (self.ring(axis, d) - self.at[axis]) * STRIDE[axis]}

    def partner(self):
        return {"dp": self.me + 1 - 2 * self.core}

    def others(self):
        return [self.partner()] + [self.near(a, d) for a in AXES for d in (LEFT, RIGHT)]

    def enter(self):
        barrier = pltpu.get_barrier_semaphore()
        for other in self.others():
            pl.semaphore_signal(barrier, inc=1, device_id=other)
        pl.semaphore_wait(barrier, 7)


def remote(src, dst, send, recv, to):
    return pltpu.make_async_remote_copy(src_ref=src, dst_ref=dst, send_sem=send, recv_sem=recv, device_id=to)


def where(c, phase, r, half, rest):
    o = ORDER[c]
    pos = {a: ALL if j < phase else (r if j == phase else rest(a)) for j, a in enumerate(o)}
    rows = cols = ALL
    if half is not None:
        if phase > 0:
            pos[o[0]] = pl.ds(2 * half, 2)
        elif c in GU:
            cols = pl.ds(FT // 2 * half, FT // 2)
        else:
            rows = pl.ds(24 * half, 16 if half else 24)
    return (*(pos[a] for a in AXES), rows, cols)


class Gather:
    def __init__(self, place, layer, ins, outs, send, recv, local):
        self.p, self.layer, self.ins, self.outs, self.send, self.recv, self.local = place, layer, ins, outs, send, recv, local

    def own(self, c, q):
        if c in GU:
            return self.ins[c], (self.layer, ALL, span(q, FT))
        return self.ins[c], (self.layer, ALL, span(q * 2 + self.p.core, LANES))

    def index(self, c, q, phase, r, half=None):
        i = where(c, phase, r, half, lambda a: self.p.at[a])
        return (q, *i[:3], self.p.core, *i[3:]) if c in GU else (q, self.p.core, *i)

    def copies(self, s, c, q):
        p, out = self.p, self.outs[c]
        sem = lambda k: (self.send.at[self.layer, q, c, k], self.recv.at[self.layer, q, c, k])
        if s == 6:
            half = out.at[q, :, :, :, p.core] if c in GU else out.at[q, p.core]
            return [remote(half, half, *sem(2 * s), p.partner())]
        phase = s // 2
        a = ORDER[c][phase]
        if s % 2 == 0:
            dst = out.at[self.index(c, q, phase, p.at[a])]
            ref, i = self.own(c, q)
            two = [(ref.at[i] if s == 0 else dst, dst)] * 2
        else:
            two = [(out.at[self.index(c, q, phase, p.ring(a, d), h)],) * 2 for h, d in enumerate((LEFT, RIGHT))]
        return [remote(*two[h], *sem(2 * s + h), p.near(a, d)) for h, d in enumerate((RIGHT, LEFT))]

    def keep(self, c, q):
        ref, i = self.own(c, q)
        return ref, i, self.outs[c], self.index(c, q, 0, self.p.at[ORDER[c][0]])

    def stage(self, s, c, q):
        if s > 0:
            for x in self.copies(s - 1, c, q): x.wait()
        if self.local is None:
            if s == 0:
                ref, i, out, j = self.keep(c, q)
                out[j] = ref[i]
        elif s in (0, 2):
            ref, i, out, j = self.keep(c, q)
            x = pltpu.make_async_copy(ref.at[i], out.at[j], self.local.at[q, c])
            x.wait() if s else x.start()
        if s < 7:
            for x in self.copies(s, c, q): x.start()


def join_down(place, w_in, peer, chip):
    first = place.core == 0
    mine, other = w_in[...].astype(f32), peer[...].astype(f32)
    chip[...] = jnp.concatenate([jnp.where(first, mine, other), jnp.where(first, other, mine)], axis=1).astype(bf16)


def fwd_kernel(x_ref, wg_in, wu_in, wd_in, h1_ref, g_hbm, u_hbm, at_hbm, wg0, wu0, wd0, wg1, wu1, wd1,
               a, act, tg, tu, td, wd, gb, ub, atb, peer, chip, send, recv, local, jsem, wsem, dsem, osem):
    place = Place()
    place.enter()
    join = remote(wd_in, peer, jsem.at[0], jsem.at[1], place.partner())
    join.start()
    ins = (wg_in, wu_in, chip)
    layers = [Gather(place, 0, ins, (tg, tu, td), send, recv, None), Gather(place, 1, ins, (wg1, wu1, wd1), send, recv, local)]

    def tick(i):
        for s in reversed(range(8)):
            for l in (1, 0):
                q = i - s - NT * l
                @pl.when((q >= 0) & (q < NT))
                def _():
                    for c in GU: layers[l].stage(s, c, q)
                if s == 0 and l == 0:
                    @pl.when(i == 0)
                    def _():
                        join.wait()
                        join_down(place, wd_in, peer, chip)
                @pl.when((q >= 0) & (q < NQ))
                def _():
                    layers[l].stage(s, DOWN, q)

    rows = T // 8
    @pl.loop(0, 8)
    def _(i):
        tick(i)
        a[span(i, rows), :] = normed(x_ref[span(i, rows), :])

    def kept(t):
        return [pltpu.make_async_copy(v.at[t], o.at[t], wsem.at[t, c]) for c, (v, o) in enumerate(((tg, wg0), (tu, wu0)))]
    def kept_down(q):
        return pltpu.make_async_copy(td.at[q], wd0.at[q], wsem.at[q, DOWN])
    def down(j):
        return pltpu.make_async_copy(wd0.at[j // 2, j % 2], wd.at[:, :, :, :, span(j, LANES)], dsem.at[j])
    def out(t, m, s):
        r = span(m, MB)
        return [pltpu.make_async_copy(gb.at[s], g_hbm.at[t, r], osem.at[0, s]),
                pltpu.make_async_copy(ub.at[s], u_hbm.at[t, r], osem.at[1, s]),
                pltpu.make_async_copy(atb.at[s], at_hbm.at[span(t, FT), r], osem.at[2, s])]

    @pl.loop(0, NT * NM)
    def _(i):
        t, m = i // NM, i % NM
        o = i % 2
        @pl.when(m == 0)
        def _():
            for x in kept(t): x.start()
            @pl.when(t == 3)
            def _():
                for q in range(NQ): kept_down(q).start()
            @pl.when(t == 4)
            def _():
                for q in range(NQ): kept_down(q).wait()
                for j in range(2 * NQ): down(j).start()
        @pl.when(i >= 2)
        def _():
            for x in out(t, m, o): x.wait()
        am = a[span(m, MB), :]
        g = dot(am, tg[t].reshape(D, FT))
        u = dot(am, tu[t].reshape(D, FT))
        gb[o] = g
        ub[o] = u
        ac = (g * jax.nn.sigmoid(g) * u).astype(bf16)
        act[span(m, MB), span(t, FT)] = ac
        atb[o] = ac.T
        for x in out(t, m, o): x.start()
        @pl.when(m == 2)
        def _():
            tick(8 + t)

    for j in range(2 * NQ): down(j).wait()
    @pl.loop(0, NM)
    def _(m):
        r = span(m, MB)
        acc = dot(act[r, :], wd[...].reshape(FF, D))
        h1_ref[r, :] = (x_ref[r, :].astype(f32) + acc.astype(bf16).astype(f32)).astype(bf16)
        tick(8 + NT + m)
    for i in (NT * NM - 2, NT * NM - 1):
        for x in out(i // NM, i % NM, i % 2): x.wait()
    for t in range(NT):
        for x in kept(t): x.wait()


VM = pl.BlockSpec(memory_space=pltpu.VMEM)
ANY = pl.BlockSpec(memory_space=pl.ANY)
DMA = pltpu.SemaphoreType.DMA


def of(dtype, *shape):
    return jax.ShapeDtypeStruct(shape, dtype)


def vm(*shape, dtype=bf16):
    return pltpu.VMEM(shape, dtype)


def forward(x, *weights):
    tiles = [of(bf16, n, *tile) for n, tile in zip(NTILES, TILE)]
    return pl.pallas_call(
        fwd_kernel, name="fwd",
        out_shape=[of(bf16, T, D), of(f32, NT, T, FT), of(f32, NT, T, FT), of(bf16, FF, T)] + tiles * 2,
        in_specs=[VM] * 4, out_specs=[VM] + [ANY] * 9,
        scratch_shapes=[vm(T, D), vm(T, FF)] + [vm(n, *tile) for n, tile in zip(NTILES, TILE)] + [
            vm(*CHIPS, 40, D), vm(2, MB, FT, dtype=f32), vm(2, MB, FT, dtype=f32), vm(2, FT, MB), vm(2, 20, D), vm(2, 40, D),
            DMA((2, NT, 3, 13)), DMA((2, NT, 3, 13)), DMA((NT, 3)), DMA((2,)), DMA((NT, 3)), DMA((2 * NQ,)), DMA((3, 2))],
        compiler_params=pltpu.CompilerParams(collective_id=0, has_side_effects=True, vmem_limit_bytes=63 << 20),
    )(x, *weights)


class Scatter:
    def __init__(self, place, c, slots, total, tile, out, sums, halves, wholes, send, recv, credit, osem=None, fin=None):
        self.p, self.c, self.slots, self.total, self.tile, self.out, self.sums = place, c, slots, total, tile, out, sums
        self.halves, self.wholes, self.send, self.recv, self.credit, self.osem, self.fin = halves, wholes, send, recv, credit, osem, fin

    def part(self, n, phase, r, half=None):
        return self.sums, (n, *where(self.c, phase, r, half, lambda a: self.p.at[a]))

    def got(self, bufs, n, phase, d, half=None):
        return bufs[phase], (n, *where(self.c, phase, d, None if phase else half, lambda a: 0))

    def final(self, q, core):
        n = NTILES[self.c]
        return (1 - q // n, ALL, span(q % n, FT) if self.c in GU else span(q % n * 2 + core, LANES))

    def copies(self, s, q):
        p, c, n = self.p, self.c, q % self.slots
        at = lambda x: x[0].at[x[1]]
        sem = lambda k: (self.send.at[n, k], self.recv.at[n, k])
        if s == 0:
            t = self.tile(q)
            return [remote(t.at[:, :, :, 1 - p.core] if c in GU else t.at[1 - p.core], self.sums.at[n], *sem(0), p.partner())]
        if s == 7:
            end = at(self.part(n, 0, p.at[ORDER[c][0]]))
            if c in GU:
                return [pltpu.make_async_copy(end, self.out.at[self.final(q, 0)], self.osem.at[n])]
            return [remote(end, self.fin.at[self.final(q, p.core)], *sem(1), p.partner())]
        phase = 2 - (s - 1) // 2
        a = ORDER[c][phase]
        ways = (RIGHT, LEFT)
        if s % 2:
            two = [(self.part(n, phase, p.ring(a, ACROSS), d), self.got(self.halves, n, phase, d, d)) for d in (0, 1)]
        else:
            two = [(self.part(n, phase, p.ring(a, ways[d])), self.got(self.wholes, n, phase, d)) for d in (0, 1)]
        return [remote(at(two[d][0]), at(two[d][1]), *sem(2 * s + d), p.near(a, ways[d])) for d in (0, 1)]

    def add(self, into, *terms):
        ref, i = into
        v = ref[i].astype(f32)
        for r, j in terms: v = v + r[j].astype(f32)
        ref[i] = v.astype(bf16)

    def stage(self, s, q):
        p, c, n = self.p, self.c, q % self.slots
        if s > 0:
            for x in self.copies(s - 1, q): x.wait()
        if s == 0:
            @pl.when(q >= self.slots)
            def _():
                for i in range(7): pl.semaphore_wait(self.credit.at[i], 1)
        elif s == 1:
            t = self.tile(q)
            @pl.loop(0, 4)
            def _(x):
                mine = t[x, :, :, p.core] if c in GU else t[p.core, x]
                self.sums[n, x] = (mine.astype(f32) + self.sums[n, x].astype(f32)).astype(bf16)
        elif s == 8:
            if c == DOWN:
                ref, j = self.part(n, 0, p.at[ORDER[c][0]])
                self.fin[self.final(q, p.core)] = ref[j]
            @pl.when(q < self.total - self.slots)
            def _():
                for i, other in enumerate(p.others()):
                    pl.semaphore_signal(self.credit.at[(0, 2, 1, 4, 3, 6, 5)[i]], inc=1, device_id=other)
        else:
            phase = 2 - (s - 2) // 2
            a = ORDER[c][phase]
            if s % 2 == 0:
                for d, way in enumerate((RIGHT, LEFT)):
                    self.add(self.part(n, phase, p.ring(a, way), d), self.got(self.halves, n, phase, d, d))
            else:
                self.add(self.part(n, phase, p.at[a]), *(self.got(self.wholes, n, phase, d) for d in (0, 1)))
        if s < 8:
            for x in self.copies(s, q): x.start()


def ring_shape(c, phase, half):
    n = {a: 4 if j < phase else (2 if j == phase else 1) for j, a in enumerate(ORDER[c])}
    if half and phase:
        n[ORDER[c][0]] = 2
    return tuple(n[a] for a in AXES) + BLOCK[c]


SLOTS = (2, 2, 3)
STEP = 6
FIRST, LATER = (1, 3, 5, 6), (1, 2, 3, 4)
EVERY, DOWN_AT = 3, (0, 1, 2, 4, 5, 6, 7, 8, 9)
DOWN1, DOWN0, LAST = 5, 8, 12


def bwd_kernel(h_hbm, dy_hbm, x_hbm, g_hbm, u_hbm, at_hbm, wg0, wu0, wd0, wg1, wu1, wd1,
               dx_hbm, at1_hbm, og, ou, od,
               a, dh, at, acc, dg, du, wg, wu, wd, ob, dob, actt, gb, ub, atb,
               wsem, gsem, bsem, dsem, xsem, *refs):
    place = Place()
    place.enter()
    refs = list(refs)
    take = lambda n: [refs.pop(0) for _ in range(n)]
    fin, = take(1)
    tiles = (lambda q: ob.at[q % 2, 0], lambda q: ob.at[q % 2, 1], lambda q: dob.at[q % NQ])
    outs = (og, ou, None)
    sc = []
    for c in range(3):
        sums, = take(1)
        sc.append(Scatter(place, c, SLOTS[c], 2 * NTILES[c], tiles[c], outs[c], sums, take(3), take(3), *take(4), fin))

    def weights(f, s):
        for l, (g_, u_, d_) in enumerate(((wg1, wu1, wd1), (wg0, wu0, wd0))):
            yield f // NT == l, [pltpu.make_async_copy(g_.at[f % NT], wg.at[s], wsem.at[0, s]), pltpu.make_async_copy(u_.at[f % NT], wu.at[s], wsem.at[1, s])] + [
                pltpu.make_async_copy(d_.at[j // 2, j % 2, span(f % NT, FT)], wd.at[s, :, span(j, LANES)], wsem.at[2 + j, s]) for j in range(2 * NQ)]
    def saved(t, m, s):
        return [pltpu.make_async_copy(g_hbm.at[t, span(m, MB)], gb.at[s], gsem.at[0, s]), pltpu.make_async_copy(u_hbm.at[t, span(m, MB)], ub.at[s], gsem.at[1, s])]
    def act_out(t, m):
        return pltpu.make_async_copy(atb, at1_hbm.at[span(t, FT), span(m, MB)], bsem)
    def act_in(src, t):
        return pltpu.make_async_copy(src.at[span(t, ROWS)], actt.at[t % 2], dsem.at[t % 2])
    def dx_out(m):
        return pltpu.make_async_copy(dh.at[span(m, MB)], dx_hbm.at[span(m, MB)], xsem.at[m])

    load_h, load_dy, load_x = (pltpu.make_async_copy(src, dst, xsem.at[i]) for i, (src, dst) in enumerate(((h_hbm, a), (dy_hbm, dh), (x_hbm, a))))
    loads = (load_h, load_dy)
    for x in loads: x.start()
    for x in next(weights(0, 0))[1]: x.start()
    for x in loads: x.wait()

    rows = 256
    @pl.loop(0, T // rows)
    def _(i):
        v = normed(a[span(i, rows), :])
        a[span(i, rows), :] = v
        at[:, span(i, rows)] = v.T

    def ff_block(layer, f, s, m):
        t, r = f % NT, span(m, MB)
        o = m % 2
        if layer:
            am = a[r, :]
            g, u = dot(am, wg[s]), dot(am, wu[s])
        else:
            for x in saved(t, m, o): x.wait()
            i = t * NM + m + 1
            @pl.when(i < NT * NM)
            def _():
                for x in saved(i // NM, i % NM, 1 - o): x.start()
            g, u = gb[o], ub[o]
        d = dot_t(dh[r, :], wd[s]).astype(bf16).astype(f32)
        sg = jax.nn.sigmoid(g)
        p = g * sg
        dgv = (d * u * (sg + p * (1 - sg))).astype(bf16)
        duv = (d * p).astype(bf16)
        dg[r, :] = dgv
        du[r, :] = duv
        if layer:
            @pl.when(f * NM + m > 0)
            def _():
                act_out(t, m).wait()
            atb[...] = (p * u).astype(bf16).T
            act_out(t, m).start()
        v = dot_t(dgv, wg[s]) + dot_t(duv, wu[s])
        @pl.when(t == 0)
        def _(): acc[r, :] = v
        @pl.when(t > 0)
        def _(): acc[r, :] += v

    def tick(S, j):
        def gate_up(s, back):
            S0 = S - back
            @pl.when((S0 >= 0) & (S0 < LAST) & (S0 != DOWN1) & (S0 != DOWN0))
            def _():
                q = S0 - (S0 > DOWN1).astype(jnp.int32) - (S0 > DOWN0).astype(jnp.int32)
                for c in GU: sc[c].stage(s, q)
        for k, i in enumerate(LATER):
            if j == i - 1: gate_up(1 + len(FIRST) + k, 2)
        for k, i in enumerate(FIRST):
            if j == i - 1: gate_up(1 + k, 1)
        if j == STEP - 1: gate_up(0, 0)
        @pl.when(S > DOWN1)
        def _():
            for s in reversed(range(9)):
                if (j - DOWN_AT[s]) % EVERY == 0:
                    for l, start in ((1, DOWN1 + 1), (0, DOWN0 + 1)):
                        d = (STEP * (S - start) + j - DOWN_AT[s]) // EVERY
                        @pl.when((d >= 0) & (d < NQ))
                        def _(): sc[DOWN].stage(s, d + NQ * (1 - l))

    @pl.loop(0, STEP * (LAST + 2))
    def _(i):
        S, j = i // STEP, i % STEP
        is_down = (S == DOWN1) | (S == DOWN0)
        is_ff = (S < LAST) & (S != DOWN1) & (S != DOWN0)
        f = S - (S > DOWN1).astype(jnp.int32) - (S > DOWN0).astype(jnp.int32)
        s = f % 2
        @pl.when(is_ff & (j == 0))
        def _():
            for ok, copies in weights(f, s):
                @pl.when(ok)
                def _():
                    for x in copies: x.wait()
            for ok, copies in weights(f + 1, 1 - s):
                @pl.when(ok & (f + 1 < 2 * NT))
                def _():
                    for x in copies: x.start()
        @pl.when((S < DOWN1) & (j < NM))
        def _():
            ff_block(1, f, s, j)
        @pl.when(is_ff & (S > DOWN1) & (j < NM))
        def _():
            ff_block(0, f, s, j)
        @pl.when(is_ff & (j >= NM))
        def _():
            r, x = span(j - NM, MB), pl.ds(2 * (j - NM), 2)
            for c, v in ((0, dg), (1, du)):
                ob[s, c, x] = dot(at[r, :], v[...]).reshape(2, *TILE[c][1:]).astype(bf16)
        @pl.when(is_down)
        def _():
            @pl.when(j == 0)
            def _():
                @pl.when(S == DOWN1)
                def _():
                    act_out(NT - 1, NM - 1).wait()
                    load_h.start()
                    act_in(at1_hbm, 0).start()
                    for x in saved(0, 0, 0): x.start()
                @pl.when(S == DOWN0)
                def _():
                    act_in(at_hbm, 0).start()
            @pl.when(j < 4)
            def _():
                act_in(at_hbm, j).wait()
                @pl.when((j < 3) & (S == DOWN1))
                def _(): act_in(at1_hbm, j + 1).start()
                @pl.when((j < 3) & (S == DOWN0))
                def _(): act_in(at_hbm, j + 1).start()
                v = dot(actt[j % 2], dh[...])
                for k in range(2 * NQ):
                    dob[k // 2, k % 2, j] = v[:, k * LANES:(k + 1) * LANES].reshape(4, 4, 40, LANES).astype(bf16)
            @pl.when((S == DOWN1) & (j == NT))
            def _():
                load_h.wait()
                @pl.loop(0, T // rows)
                def _(i):
                    r = span(i, rows)
                    dh[r, :] = norm_back(a[r, :], acc[r, :], dh[r, :])
                load_x.start()
                load_x.wait()
                @pl.loop(0, T // rows)
                def _(i):
                    at[:, span(i, rows)] = normed(a[span(i, rows), :]).T
        @pl.when((S == LAST) & (j < NM))
        def _():
            r = span(j, MB)
            dh[r, :] = norm_back(a[r, :], acc[r, :], dh[r, :])
            dx_out(j).start()
        for k in range(STEP):
            @pl.when(j == k)
            def _(): tick(S, k)
    first = place.core == 0
    v = fin[...].astype(f32)
    od[...] = jnp.where(first, v[:, :20], v[:, 20:]).astype(bf16)
    for m in range(NM): dx_out(m).wait()


def backward(h1, dy, x, g, u, at, *tiles):
    two = [t.reshape((NT, D, FT) if c in GU else (NQ, 2, FF, LANES)) for t, c in zip(tiles, (0, 1, 2) * 2)]
    rings = []
    for c in range(3):
        rings += [vm(SLOTS[c], *CHIPS, *BLOCK[c])] + [vm(SLOTS[c], *ring_shape(c, ph, half)) for half in (True, False) for ph in range(3)] + [DMA((SLOTS[c], 18)), DMA((SLOTS[c], 18)), pltpu.SemaphoreType.REGULAR((7,)), DMA((SLOTS[c],))]
    return pl.pallas_call(
        bwd_kernel, name="bwd",
        out_shape=[of(bf16, T, D), of(bf16, FF, T), of(bf16, 2, 8, FF), of(bf16, 2, 8, FF), of(bf16, 2, 20, D)],
        in_specs=[ANY] * 12, out_specs=[ANY] * 4 + [VM],
        scratch_shapes=[vm(T, D), vm(T, D), vm(D, T), vm(T, D, dtype=f32), vm(T, FT), vm(T, FT), vm(2, D, FT), vm(2, D, FT), vm(2, FT, D),
                        vm(2, 2, *TILE[0]), vm(NQ, *TILE[DOWN]), vm(2, ROWS, T), vm(2, MB, FT, dtype=f32), vm(2, MB, FT, dtype=f32), vm(FT, MB),
                        DMA((10, 2)), DMA((2, 2)), DMA, DMA((2,)), DMA((NM,)), vm(2, 40, D)] + rings,
        compiler_params=pltpu.CompilerParams(collective_id=1, has_side_effects=True, vmem_limit_bytes=(64 << 20) - (64 << 10)),
    )(h1, dy, x, g, u, at, *two)


def solution(mesh):
    def step(x, dy, *weights):
        h1, g, u, at, *tiles = forward(x[0], *weights)
        dx, _, *grads = backward(h1, dy[0], x[0], g, u, at, *tiles)
        return (dx[None], *grads)

    tokens, rows = P(("rep", "dp")), P(None, "dp", None)
    return jax.shard_map(step, mesh=mesh, in_specs=(tokens, tokens, rows, rows, rows), out_specs=(tokens,) + (P("rep", "dp", None),) * 3, check_vma=False)
```

time: 3080 us -> 416 us (0.14)
  waiting for transfers between devices: 2140 us -> 0 us
  Pallas kernels: 0 us -> 406 us
  blocking collectives: 370 us -> 0 us
  matrix products: 316 us -> 0 us
  starting transfers between devices: 117 us -> 0 us
  other arithmetic: 68 us -> 0 us
  local copies, waits for them, and re-layouts: 46.1 us -> 9.11 us
    unnamed x58 -> x0, waiting for transfers between devices: 1870 us -> none
    pallas_call x0 -> x2, Pallas kernels: none -> 406 us  [the longest x1 298 us: backward(): pl.pallas_call(bwd_kernel, name='bwd', out_shape=[of(bf16, T, D), of(bf16...]
    unnamed x1 -> x0, blocking collectives: 370 us -> none
    dot_general x17 -> x0, matrix products: 316 us -> none  [the longest x6 115 us: layer(): up = jnp.dot(a, w['w_up'], preferred_element_type=jnp.float32)]
    squeeze x6 -> x0, waiting for transfers between devices: 270 us -> none  [stack(): h = layer(h, {name: w[number] for name, w in weights.items()})]
    unnamed x48 -> x0, starting transfers between devices: 117 us -> none
    unnamed x5 -> x0, other arithmetic: 52 us -> none
    unnamed x40 -> x9, local copies, waits for them, and re-layouts: 41.4 us -> 9.11 us
  transfers between devices with their start and end apart: 54 -> 0, of which waited for: 9 -> 0; matrix products, arithmetic and copies ran while one was open for 25% -> 0% of each run, Pallas kernels for 0% -> 0%
where the time goes in v2:
time: 416 us
  Pallas kernels  406 us (98%)
  local copies, waits for them, and re-layouts  9.11 us (2%)
    pallas_call x1, Pallas kernels, backward(): pl.pallas_call(bwd_kernel, name='bwd', out_shape=[of(bf16, T, D), of(bf16...  298 us
    pallas_call x1, Pallas kernels, forward(): pl.pallas_call(fwd_kernel, name='fwd', out_shape=[of(bf16, T, D), of(f32,...  108 us
    unnamed x9, local copies, waits for them, and re-layouts  9.11 us

profile of v2, /device:TPU:0, one launch (start us, length us, event | category | flops | bytes accessed | tf_op | source)
XLA Modules:
  0.0 416.1 jit_solution(12607327322395731951)
XLA Ops:
  0.6 1.5 copy.9.wd_in
  2.2 108.2 %fwd.1 = (bf16[2048,1024]{1,0:T(8,128)(2,1)}, f32[5,2048,512]{2,1,0:T(8,128)}, f32[5,2048,512]{2,1,0:T(8,128)}, bf16[2560,2048]{1,0:T(8,128)(2,1)}, bf16[5,4,4,4...) custom-call(bf16[2048,1024]{1,0:T(8,128)(2,1)} %bitcast.9, ...), custom_call_target="tpu_custom_call" | custom-call | tf_op jit(solution)/shard_map/fwd/pallas_call | solution.py:254
  110.4 298.1 %bwd.1 = (bf16[2048,1024]{1,0:T(8,128)(2,1)}, bf16[2560,2048]{1,0:T(8,128)(2,1)}, bf16[2,8,2560]{2,1,0:T(8,128)(2,1)}, bf16[2,8,2560]{2,1,0:T(8,128)(2,1)}, bf16[2,20,1024]{2,1,0:T(8,128)(2,1)}) custom-call(bf16[2048,1024]{1,0:T(8,128)(2,1)} %get-tuple-element.18.h_hbm, bf16[2048,1024]{1,0:T(8,128)(2,1)} %bitcast.17, bf16[2048,1024]{1,0:T(8,128)(2,1)} %bitcast.10, ...), custom_call_target="tpu_custom_call" | custom-call | tf_op jit(solution)/shard_map/bwd/pallas_call | solution.py:532
  408.5 0.0 copy-start.1
  408.5 0.0 copy-start
  408.5 1.6 copy.10
  410.2 4.6 %copy.14 = bf16[1,2048,1024]{2,1,0:T(8,128)(2,1)} copy(bf16[1,2048,1024]{2,1,0:T(8,128)(2,1)} %bitcast.18) | data formatting | bytes 8388608
  414.8 0.0 copy-done.1
  414.8 0.6 copy.15
  415.4 0.0 copy-done
  415.4 0.6 copy.16
Async XLA Ops:
  408.5 6.3 %copy-start.1 = (bf16[2,8,2560]{2,1,0:T(8,128)(2,1)S(1)}, bf16[2,8,2560]{2,1,0:T(8,128)(2,1)}, u32[]{:S(2)}) copy-start(bf16[2,8,2560]{2,1,0:T(8,128)(2,1)} %get-tuple-element.41) | copy-start | bytes 245764
  408.5 6.9 %copy-start = (bf16[2,8,2560]{2,1,0:T(8,128)(2,1)S(1)}, bf16[2,8,2560]{2,1,0:T(8,128)(2,1)}, u32[]{:S(2)}) copy-start(bf16[2,8,2560]{2,1,0:T(8,128)(2,1)} %get-tuple-element.42) | copy-start | bytes 245764

commit v3 on v2

--- a/solution.py
+++ b/solution.py
@@ -1,4 +1,4 @@
-import functools
+import functools, itertools
 import jax, jax.numpy as jnp
 from jax import lax
 from jax.experimental import pallas as pl
@@ -10,6 +10,7 @@
 NT, FT = 5, 512
 NQ, LANES = 4, 128
 MB = 512
+SUBS = 1
 NM = T // MB
 ROWS = FF // 4
 AXES = ("x", "y", "z")
@@ -62,85 +63,94 @@
     def ring(self, axis, d):
         return (self.at[axis] + d) % 4
 
-    def near(self, axis, d):
-        return {"dp": self.me + (self.ring(axis, d) - self.at[axis]) * STRIDE[axis]}
+    def shifted(self, *moves):
+        return {"dp": self.me + sum((self.ring(a, d) - self.at[a]) * STRIDE[a] for a, d in moves)}
 
     def partner(self):
         return {"dp": self.me + 1 - 2 * self.core}
 
-    def others(self):
-        return [self.partner()] + [self.near(a, d) for a in AXES for d in (LEFT, RIGHT)]
+    def in_plane(self, c, k, way=1):
+        return tuple(zip(ORDER[c][:2], (way * (k // 4) % 4, way * (k % 4) % 4)))
 
     def enter(self):
         barrier = pltpu.get_barrier_semaphore()
-        for other in self.others():
-            pl.semaphore_signal(barrier, inc=1, device_id=other)
-        pl.semaphore_wait(barrier, 7)
+        moves = [m for m in itertools.product(range(4), repeat=3) if 0 in m and any(m)]
+        for m in moves:
+            pl.semaphore_signal(barrier, inc=1, device_id=self.shifted(*zip(AXES, m)))
+        pl.semaphore_signal(barrier, inc=1, device_id=self.partner())
+        pl.semaphore_wait(barrier, len(moves) + 1)
+
+
+PEERS = range(1, 16)
 
 
 def remote(src, dst, send, recv, to):
     return pltpu.make_async_remote_copy(src_ref=src, dst_ref=dst, send_sem=send, recv_sem=recv, device_id=to)
 
 
-def where(c, phase, r, half, rest):
+def block(c, place, moves=()):
+    pos = dict(moves)
+    return tuple(place.ring(a, pos[a]) if a in pos else place.at[a] for a in AXES)
+
+
+def plane(c, r, half=None):
     o = ORDER[c]
-    pos = {a: ALL if j < phase else (r if j == phase else rest(a)) for j, a in enumerate(o)}
-    rows = cols = ALL
-    if half is not None:
-        if phase > 0:
-            pos[o[0]] = pl.ds(2 * half, 2)
-        elif c in GU:
-            cols = pl.ds(FT // 2 * half, FT // 2)
-        else:
-            rows = pl.ds(24 * half, 16 if half else 24)
-    return (*(pos[a] for a in AXES), rows, cols)
+    pos = {o[0]: ALL if half is None else pl.ds(2 * half, 2), o[1]: ALL, o[2]: r}
+    return tuple(pos[a] for a in AXES)
+
+
+def joint(place, buf, sem):
+    return remote(buf, buf, *sem, place.partner())
 
 
 class Gather:
-    def __init__(self, place, layer, ins, outs, send, recv, local):
-        self.p, self.layer, self.ins, self.outs, self.send, self.recv, self.local = place, layer, ins, outs, send, recv, local
+    STAGES = 5
+
+    def __init__(self, place, layer, ins, outs, size, send, recv, local):
+        self.p, self.layer, self.ins, self.outs, self.size = place, layer, ins, outs, size
+        self.send, self.recv, self.local = send, recv, local
 
     def own(self, c, q):
         if c in GU:
             return self.ins[c], (self.layer, ALL, span(q, FT))
         return self.ins[c], (self.layer, ALL, span(q * 2 + self.p.core, LANES))
 
-    def index(self, c, q, phase, r, half=None):
-        i = where(c, phase, r, half, lambda a: self.p.at[a])
-        return (q, *i[:3], self.p.core, *i[3:]) if c in GU else (q, self.p.core, *i)
+    def index(self, c, q, i):
+        return (q, *i, self.p.core) if c in GU else (q, self.p.core, *i)
+
+    def sem(self, c, q, k):
+        return self.send.at[self.layer, q, c, k], self.recv.at[self.layer, q, c, k]
 
     def copies(self, s, c, q):
         p, out = self.p, self.outs[c]
-        sem = lambda k: (self.send.at[self.layer, q, c, k], self.recv.at[self.layer, q, c, k])
-        if s == 6:
-            half = out.at[q, :, :, :, p.core] if c in GU else out.at[q, p.core]
-            return [remote(half, half, *sem(2 * s), p.partner())]
-        phase = s // 2
-        a = ORDER[c][phase]
-        if s % 2 == 0:
-            dst = out.at[self.index(c, q, phase, p.at[a])]
+        sem = functools.partial(self.sem, c, q)
+        if s == 0:
             ref, i = self.own(c, q)
-            two = [(ref.at[i] if s == 0 else dst, dst)] * 2
+            return [remote(ref.at[i], out.at[self.index(c, q, block(c, p))], *sem(0), p.shifted(*p.in_plane(c, k))) for k in PEERS]
+        if s == 3:
+            half = out.at[self.index(c, q, (ALL,) * 3)]
+            return [remote(half, half, *sem(5), p.partner())]
+        a = ORDER[c][2]
+        if s == 1:
+            whole = [out.at[self.index(c, q, plane(c, p.at[a]))]] * 2
         else:
-            two = [(out.at[self.index(c, q, phase, p.ring(a, d), h)],) * 2 for h, d in enumerate((LEFT, RIGHT))]
-        return [remote(*two[h], *sem(2 * s + h), p.near(a, d)) for h, d in enumerate((RIGHT, LEFT))]
-
-    def keep(self, c, q):
+            whole = [out.at[self.index(c, q, plane(c, p.ring(a, d), h))] for h, d in enumerate((LEFT, RIGHT))]
+        return [remote(whole[h], whole[h], *sem(2 * s - 1 + h), p.shifted((a, d))) for h, d in enumerate((RIGHT, LEFT))]
+
+    def stage(self, s, c, q):
         ref, i = self.own(c, q)
-        return ref, i, self.outs[c], self.index(c, q, 0, self.p.at[ORDER[c][0]])
-
-    def stage(self, s, c, q):
-        if s > 0:
+        keep = (self.outs[c], self.index(c, q, block(c, self.p)))
+        if s == 1:
+            joint(self.p, self.size[c], self.sem(c, q, 0)).wait()
+        elif s > 1:
             for x in self.copies(s - 1, c, q): x.wait()
         if self.local is None:
             if s == 0:
-                ref, i, out, j = self.keep(c, q)
-                out[j] = ref[i]
-        elif s in (0, 2):
-            ref, i, out, j = self.keep(c, q)
-            x = pltpu.make_async_copy(ref.at[i], out.at[j], self.local.at[q, c])
+                keep[0][keep[1]] = ref[i]
+        elif s < 2:
+            x = pltpu.make_async_copy(ref.at[i], keep[0].at[keep[1]], self.local.at[q, c])
             x.wait() if s else x.start()
-        if s < 7:
+        if s < 4:
             for x in self.copies(s, c, q): x.start()
 
 
@@ -150,19 +160,24 @@
     chip[...] = jnp.concatenate([jnp.where(first, mine, other), jnp.where(first, other, mine)], axis=1).astype(bf16)
 
 
+APART = 2
+READY0 = APART * 4
+
+
 def fwd_kernel(x_ref, wg_in, wu_in, wd_in, h1_ref, g_hbm, u_hbm, at_hbm, wg0, wu0, wd0, wg1, wu1, wd1,
-               a, act, tg, tu, td, wd, gb, ub, atb, peer, chip, send, recv, local, jsem, wsem, dsem, osem):
+               a, act, tg, tu, td, wd, gb, ub, atb, peer, chip, size_gu, size_down, send, recv, local, jsem, wsem, dsem, osem):
     place = Place()
     place.enter()
     join = remote(wd_in, peer, jsem.at[0], jsem.at[1], place.partner())
     join.start()
     ins = (wg_in, wu_in, chip)
-    layers = [Gather(place, 0, ins, (tg, tu, td), send, recv, None), Gather(place, 1, ins, (wg1, wu1, wd1), send, recv, local)]
+    size = (size_gu, size_gu, size_down)
+    layers = [Gather(place, 0, ins, (tg, tu, td), size, send, recv, None), Gather(place, 1, ins, (wg1, wu1, wd1), size, send, recv, local)]
 
     def tick(i):
-        for s in reversed(range(8)):
+        for s in reversed(range(Gather.STAGES)):
             for l in (1, 0):
-                q = i - s - NT * l
+                q = i - APART * s - NT * l
                 @pl.when((q >= 0) & (q < NT))
                 def _():
                     for c in GU: layers[l].stage(s, c, q)
@@ -178,8 +193,10 @@
     rows = T // 8
     @pl.loop(0, 8)
     def _(i):
-        tick(i)
+        @pl.when(i <= READY0)
+        def _(): tick(i)
         a[span(i, rows), :] = normed(x_ref[span(i, rows), :])
+    for i in range(8, READY0 + 1): tick(i)
 
     def kept(t):
         return [pltpu.make_async_copy(v.at[t], o.at[t], wsem.at[t, c]) for c, (v, o) in enumerate(((tg, wg0), (tu, wu0)))]
@@ -221,7 +238,7 @@
         for x in out(t, m, o): x.start()
         @pl.when(m == 2)
         def _():
-            tick(8 + t)
+            tick(READY0 + 1 + t)
 
     for j in range(2 * NQ): down(j).wait()
     @pl.loop(0, NM)
@@ -229,7 +246,10 @@
         r = span(m, MB)
         acc = dot(act[r, :], wd[...].reshape(FF, D))
         h1_ref[r, :] = (x_ref[r, :].astype(f32) + acc.astype(bf16).astype(f32)).astype(bf16)
-        tick(8 + NT + m)
+        tick(READY0 + 1 + NT + m)
+    @pl.loop(READY0 + 1 + NT + NM, READY0 + 2 * NT)
+    def _(i):
+        tick(i)
     for i in (NT * NM - 2, NT * NM - 1):
         for x in out(i // NM, i % NM, i % 2): x.wait()
     for t in range(NT):
@@ -256,99 +276,93 @@
         out_shape=[of(bf16, T, D), of(f32, NT, T, FT), of(f32, NT, T, FT), of(bf16, FF, T)] + tiles * 2,
         in_specs=[VM] * 4, out_specs=[VM] + [ANY] * 9,
         scratch_shapes=[vm(T, D), vm(T, FF)] + [vm(n, *tile) for n, tile in zip(NTILES, TILE)] + [
-            vm(*CHIPS, 40, D), vm(2, MB, FT, dtype=f32), vm(2, MB, FT, dtype=f32), vm(2, FT, MB), vm(2, 20, D), vm(2, 40, D),
-            DMA((2, NT, 3, 13)), DMA((2, NT, 3, 13)), DMA((NT, 3)), DMA((2,)), DMA((NT, 3)), DMA((2 * NQ,)), DMA((3, 2))],
+            vm(*CHIPS, 40, D), vm(2, MB, FT, dtype=f32), vm(2, MB, FT, dtype=f32), vm(2, FT, MB), vm(2, 20, D), vm(2, 40, D), vm(15, *BLOCK[0]), vm(15, *BLOCK[DOWN]),
+            DMA((2, NT, 3, 6)), DMA((2, NT, 3, 6)), DMA((NT, 3)), DMA((2,)), DMA((NT, 3)), DMA((2 * NQ,)), DMA((3, 2))],
         compiler_params=pltpu.CompilerParams(collective_id=0, has_side_effects=True, vmem_limit_bytes=63 << 20),
     )(x, *weights)
 
 
 class Scatter:
-    def __init__(self, place, c, slots, total, tile, out, sums, halves, wholes, send, recv, credit, osem=None, fin=None):
-        self.p, self.c, self.slots, self.total, self.tile, self.out, self.sums = place, c, slots, total, tile, out, sums
-        self.halves, self.wholes, self.send, self.recv, self.credit, self.osem, self.fin = halves, wholes, send, recv, credit, osem, fin
-
-    def part(self, n, phase, r, half=None):
-        return self.sums, (n, *where(self.c, phase, r, half, lambda a: self.p.at[a]))
-
-    def got(self, bufs, n, phase, d, half=None):
-        return bufs[phase], (n, *where(self.c, phase, d, None if phase else half, lambda a: 0))
+    STAGES = 6
+
+    def __init__(self, place, c, slots, total, tile, out, fin, sums, halves, wholes, blocks, send, recv, credit, osem):
+        self.p, self.c, self.slots, self.total, self.tile, self.out, self.fin = place, c, slots, total, tile, out, fin
+        self.sums, self.halves, self.wholes, self.blocks = sums, halves, wholes, blocks
+        self.send, self.recv, self.credit, self.osem = send, recv, credit, osem
 
     def final(self, q, core):
         n = NTILES[self.c]
         return (1 - q // n, ALL, span(q % n, FT) if self.c in GU else span(q % n * 2 + core, LANES))
 
+    def sem(self, q, k):
+        return self.send.at[q % self.slots, k], self.recv.at[q % self.slots, k]
+
     def copies(self, s, q):
         p, c, n = self.p, self.c, q % self.slots
-        at = lambda x: x[0].at[x[1]]
-        sem = lambda k: (self.send.at[n, k], self.recv.at[n, k])
+        sem = functools.partial(self.sem, q)
         if s == 0:
             t = self.tile(q)
             return [remote(t.at[:, :, :, 1 - p.core] if c in GU else t.at[1 - p.core], self.sums.at[n], *sem(0), p.partner())]
-        if s == 7:
-            end = at(self.part(n, 0, p.at[ORDER[c][0]]))
+        if s == 3:
+            ways = [(k, p.in_plane(c, k, -1)) for k in PEERS]
+            return [remote(self.sums.at[(n, *block(c, p, m))], self.blocks.at[n, k - 1], *sem(5), p.shifted(*m)) for k, m in ways]
+        if s == 4:
+            end = self.sums.at[(n, *block(c, p))]
             if c in GU:
                 return [pltpu.make_async_copy(end, self.out.at[self.final(q, 0)], self.osem.at[n])]
-            return [remote(end, self.fin.at[self.final(q, p.core)], *sem(1), p.partner())]
-        phase = 2 - (s - 1) // 2
-        a = ORDER[c][phase]
+            return [remote(end, self.fin.at[self.final(q, p.core)], *sem(6), p.partner())]
+        a = ORDER[c][2]
         ways = (RIGHT, LEFT)
-        if s % 2:
-            two = [(self.part(n, phase, p.ring(a, ACROSS), d), self.got(self.halves, n, phase, d, d)) for d in (0, 1)]
+        if s == 1:
+            two = [(self.sums.at[(n, *plane(c, p.ring(a, ACROSS), d))], self.halves.at[n, d]) for d in (0, 1)]
         else:
-            two = [(self.part(n, phase, p.ring(a, ways[d])), self.got(self.wholes, n, phase, d)) for d in (0, 1)]
-        return [remote(at(two[d][0]), at(two[d][1]), *sem(2 * s + d), p.near(a, ways[d])) for d in (0, 1)]
-
-    def add(self, into, *terms):
-        ref, i = into
-        v = ref[i].astype(f32)
-        for r, j in terms: v = v + r[j].astype(f32)
-        ref[i] = v.astype(bf16)
+            two = [(self.sums.at[(n, *plane(c, p.ring(a, ways[d])))], self.wholes.at[n, d]) for d in (0, 1)]
+        return [remote(*two[d], *sem(2 * s - 1 + d), p.shifted((a, ways[d]))) for d in (0, 1)]
+
+    def add(self, i, *terms):
+        v = self.sums[i].astype(f32)
+        for t in terms: v = v + t.astype(f32)
+        self.sums[i] = v.astype(bf16)
 
     def stage(self, s, q):
         p, c, n = self.p, self.c, q % self.slots
-        if s > 0:
+        a = ORDER[c][2]
+        if s == 4:
+            joint(p, self.blocks.at[n], self.sem(q, 5)).wait()
+        elif s > 0:
             for x in self.copies(s - 1, q): x.wait()
         if s == 0:
             @pl.when(q >= self.slots)
             def _():
-                for i in range(7): pl.semaphore_wait(self.credit.at[i], 1)
+                for i in range(18): pl.semaphore_wait(self.credit.at[i], 1)
         elif s == 1:
             t = self.tile(q)
             @pl.loop(0, 4)
             def _(x):
-                mine = t[x, :, :, p.core] if c in GU else t[p.core, x]
-                self.sums[n, x] = (mine.astype(f32) + self.sums[n, x].astype(f32)).astype(bf16)
-        elif s == 8:
+                self.add((n, x), t[x, :, :, p.core] if c in GU else t[p.core, x])
+        elif s == 2:
+            for d, way in enumerate((RIGHT, LEFT)):
+                self.add((n, *plane(c, p.ring(a, way), d)), self.halves[n, d])
+        elif s == 3:
+            self.add((n, *plane(c, p.at[a])), self.wholes[n, 0], self.wholes[n, 1])
+        elif s == 4:
+            self.add((n, *block(c, p)), *(self.blocks[n, k - 1] for k in PEERS))
+        else:
             if c == DOWN:
-                ref, j = self.part(n, 0, p.at[ORDER[c][0]])
-                self.fin[self.final(q, p.core)] = ref[j]
+                self.fin[self.final(q, p.core)] = self.sums[(n, *block(c, p))]
             @pl.when(q < self.total - self.slots)
             def _():
-                for i, other in enumerate(p.others()):
-                    pl.semaphore_signal(self.credit.at[(0, 2, 1, 4, 3, 6, 5)[i]], inc=1, device_id=other)
-        else:
-            phase = 2 - (s - 2) // 2
-            a = ORDER[c][phase]
-            if s % 2 == 0:
-                for d, way in enumerate((RIGHT, LEFT)):
-                    self.add(self.part(n, phase, p.ring(a, way), d), self.got(self.halves, n, phase, d, d))
-            else:
-                self.add(self.part(n, phase, p.at[a]), *(self.got(self.wholes, n, phase, d) for d in (0, 1)))
-        if s < 8:
+                others = [p.partner(), p.shifted((a, LEFT)), p.shifted((a, RIGHT))] + [p.shifted(*p.in_plane(c, k)) for k in PEERS]
+                for i, other in enumerate(others):
+                    pl.semaphore_signal(self.credit.at[i], inc=1, device_id=other)
+        if s < 5:
             for x in self.copies(s, q): x.start()
-
-
-def ring_shape(c, phase, half):
-    n = {a: 4 if j < phase else (2 if j == phase else 1) for j, a in enumerate(ORDER[c])}
-    if half and phase:
-        n[ORDER[c][0]] = 2
-    return tuple(n[a] for a in AXES) + BLOCK[c]
 
 
 SLOTS = (2, 2, 3)
 STEP = 6
-FIRST, LATER = (1, 3, 5, 6), (1, 2, 3, 4)
-EVERY, DOWN_AT = 3, (0, 1, 2, 4, 5, 6, 7, 8, 9)
+FIRST, LATER = (1, 3, 5), (2, 4)
+EVERY, DOWN_AT = 3, (0, 1, 3, 5, 7, 8)
 DOWN1, DOWN0, LAST = 5, 8, 12
 
 
@@ -365,8 +379,7 @@
     outs = (og, ou, None)
     sc = []
     for c in range(3):
-        sums, = take(1)
-        sc.append(Scatter(place, c, SLOTS[c], 2 * NTILES[c], tiles[c], outs[c], sums, take(3), take(3), *take(4), fin))
+        sc.append(Scatter(place, c, SLOTS[c], 2 * NTILES[c], tiles[c], outs[c], fin, *take(8)))
 
     def weights(f, s):
         for l, (g_, u_, d_) in enumerate(((wg1, wu1, wd1), (wg0, wu0, wd0))):
@@ -395,36 +408,38 @@
         at[:, span(i, rows)] = v.T
 
     def ff_block(layer, f, s, m):
-        t, r = f % NT, span(m, MB)
-        o = m % 2
+        t, o = f % NT, m % 2
+        n = MB // SUBS
+        rows = [pl.ds(mult(m * MB + n * k, n), n) for k in range(SUBS)]
         if layer:
-            am = a[r, :]
-            g, u = dot(am, wg[s]), dot(am, wu[s])
+            gu = [(dot(a[r, :], wg[s]), dot(a[r, :], wu[s])) for r in rows]
         else:
             for x in saved(t, m, o): x.wait()
             i = t * NM + m + 1
             @pl.when(i < NT * NM)
             def _():
                 for x in saved(i // NM, i % NM, 1 - o): x.start()
-            g, u = gb[o], ub[o]
-        d = dot_t(dh[r, :], wd[s]).astype(bf16).astype(f32)
-        sg = jax.nn.sigmoid(g)
-        p = g * sg
-        dgv = (d * u * (sg + p * (1 - sg))).astype(bf16)
-        duv = (d * p).astype(bf16)
-        dg[r, :] = dgv
-        du[r, :] = duv
+            gu = [(gb[o, n * k:n * k + n], ub[o, n * k:n * k + n]) for k in range(SUBS)]
         if layer:
             @pl.when(f * NM + m > 0)
             def _():
                 act_out(t, m).wait()
-            atb[...] = (p * u).astype(bf16).T
+        ds = [dot_t(dh[r, :], wd[s]).astype(bf16).astype(f32) for r in rows]
+        back = []
+        for k, (r, (g, u), d) in enumerate(zip(rows, gu, ds)):
+            sg = jax.nn.sigmoid(g)
+            p = g * sg
+            dgv = (d * u * (sg + p * (1 - sg))).astype(bf16)
+            duv = (d * p).astype(bf16)
+            dg[r, :] = dgv
+            du[r, :] = duv
+            if layer:
+                atb[:, n * k:n * k + n] = (p * u).astype(bf16).T
+            back.append((dgv, duv))
+        for r, (dgv, duv) in zip(rows, back):
+            acc[r, :] += dot_t(dgv, wg[s]) + dot_t(duv, wu[s])
+        if layer:
             act_out(t, m).start()
-        v = dot_t(dgv, wg[s]) + dot_t(duv, wu[s])
-        @pl.when(t == 0)
-        def _(): acc[r, :] = v
-        @pl.when(t > 0)
-        def _(): acc[r, :] += v
 
     def tick(S, j):
         def gate_up(s, back):
@@ -434,13 +449,13 @@
                 q = S0 - (S0 > DOWN1).astype(jnp.int32) - (S0 > DOWN0).astype(jnp.int32)
                 for c in GU: sc[c].stage(s, q)
         for k, i in enumerate(LATER):
-            if j == i - 1: gate_up(1 + len(FIRST) + k, 2)
+            if j == i: gate_up(1 + len(FIRST) + k, 2)
         for k, i in enumerate(FIRST):
-            if j == i - 1: gate_up(1 + k, 1)
+            if j == i: gate_up(1 + k, 1)
         if j == STEP - 1: gate_up(0, 0)
         @pl.when(S > DOWN1)
         def _():
-            for s in reversed(range(9)):
+            for s in reversed(range(Scatter.STAGES)):
                 if (j - DOWN_AT[s]) % EVERY == 0:
                     for l, start in ((1, DOWN1 + 1), (0, DOWN0 + 1)):
                         d = (STEP * (S - start) + j - DOWN_AT[s]) // EVERY
@@ -456,6 +471,9 @@
         s = f % 2
         @pl.when(is_ff & (j == 0))
         def _():
+            @pl.when(f % NT == 0)
+            def _():
+                acc[...] = jnp.zeros_like(acc)
             for ok, copies in weights(f, s):
                 @pl.when(ok)
                 def _():
@@ -528,7 +546,10 @@
     two = [t.reshape((NT, D, FT) if c in GU else (NQ, 2, FF, LANES)) for t, c in zip(tiles, (0, 1, 2) * 2)]
     rings = []
     for c in range(3):
-        rings += [vm(SLOTS[c], *CHIPS, *BLOCK[c])] + [vm(SLOTS[c], *ring_shape(c, ph, half)) for half in (True, False) for ph in range(3)] + [DMA((SLOTS[c], 18)), DMA((SLOTS[c], 18)), pltpu.SemaphoreType.REGULAR((7,)), DMA((SLOTS[c],))]
+        n = SLOTS[c]
+        flat = [4 // (1 + (ORDER[c][0] == x)) for x in AXES if x != ORDER[c][2]]
+        rings += [vm(n, *CHIPS, *BLOCK[c]), vm(n, 2, *flat, *BLOCK[c]), vm(n, 2, 4, 4, *BLOCK[c]), vm(n, 15, *BLOCK[c]),
+                  DMA((n, 7)), DMA((n, 7)), pltpu.SemaphoreType.REGULAR((18,)), DMA((n,))]
     return pl.pallas_call(
         bwd_kernel, name="bwd",
         out_shape=[of(bf16, T, D), of(bf16, FF, T), of(bf16, 2, 8, FF), of(bf16, 2, 8, FF), of(bf16, 2, 20, D)],

time: 416 us -> 375 us (0.901)
  Pallas kernels: 406 us -> 365 us
    pallas_call x1, Pallas kernels: 298 us -> 254 us  [backward(): pl.pallas_call(bwd_kernel, name='bwd', out_shape=[of(bf16, T, D), of(bf16...]
where the time goes in v3:
time: 375 us; the launch traced here: 374 us
  Pallas kernels  365 us (97%)
  local copies, waits for them, and re-layouts  9.11 us (2%)
    pallas_call x1, Pallas kernels, backward(): pl.pallas_call(bwd_kernel, name='bwd', out_shape=[of(bf16, T, D), of(bf16...  254 us
    pallas_call x1, Pallas kernels, forward(): pl.pallas_call(fwd_kernel, name='fwd', out_shape=[of(bf16, T, D), of(f32,...  111 us
    unnamed x9, local copies, waits for them, and re-layouts  9.11 us

profile of v3, /device:TPU:0, one launch (start us, length us, event | category | flops | bytes accessed | tf_op | source)
XLA Modules:
  0.0 374.5 jit_solution(15541680414448216623)
XLA Ops:
  0.6 1.5 copy.9.wd_in
  2.2 111.0 %fwd.1 = (bf16[2048,1024]{1,0:T(8,128)(2,1)}, f32[5,2048,512]{2,1,0:T(8,128)}, f32[5,2048,512]{2,1,0:T(8,128)}, bf16[2560,2048]{1,0:T(8,128)(2,1)}, bf16[5,4,4,4...) custom-call(bf16[2048,1024]{1,0:T(8,128)(2,1)} %bitcast.9, ...), custom_call_target="tpu_custom_call" | custom-call | tf_op jit(solution)/shard_map/fwd/pallas_call | solution.py:274
  113.2 253.7 %bwd.1 = (bf16[2048,1024]{1,0:T(8,128)(2,1)}, bf16[2560,2048]{1,0:T(8,128)(2,1)}, bf16[2,8,2560]{2,1,0:T(8,128)(2,1)}, bf16[2,8,2560]{2,1,0:T(8,128)(2,1)}, bf16[2,20,1024]{2,1,0:T(8,128)(2,1)}) custom-call(bf16[2048,1024]{1,0:T(8,128)(2,1)} %get-tuple-element.18.h_hbm, bf16[2048,1024]{1,0:T(8,128)(2,1)} %bitcast.17, bf16[2048,1024]{1,0:T(8,128)(2,1)} %bitcast.10, ...), custom_call_target="tpu_custom_call" | custom-call | tf_op jit(solution)/shard_map/bwd/pallas_call | solution.py:553
  366.9 0.0 copy-start.1
  366.9 0.0 copy-start
  366.9 1.6 copy.10
  368.6 4.6 %copy.14 = bf16[1,2048,1024]{2,1,0:T(8,128)(2,1)} copy(bf16[1,2048,1024]{2,1,0:T(8,128)(2,1)} %bitcast.18) | data formatting | bytes 8388608
  373.2 0.0 copy-done.1
  373.2 0.6 copy.15
  373.8 0.0 copy-done
  373.9 0.6 copy.16
Async XLA Ops:
  366.9 6.3 %copy-start.1 = (bf16[2,8,2560]{2,1,0:T(8,128)(2,1)S(1)}, bf16[2,8,2560]{2,1,0:T(8,128)(2,1)}, u32[]{:S(2)}) copy-start(bf16[2,8,2560]{2,1,0:T(8,128)(2,1)} %get-tuple-element.41) | copy-start | bytes 245764
  366.9 6.9 %copy-start = (bf16[2,8,2560]{2,1,0:T(8,128)(2,1)S(1)}, bf16[2,8,2560]{2,1,0:T(8,128)(2,1)}, u32[]{:S(2)}) copy-start(bf16[2,8,2560]{2,1,0:T(8,128)(2,1)} %get-tuple-element.42) | copy-start | bytes 245764

commit v4 on v3

v4 whole, which is shorter than its diff:
```python
import functools, itertools
import jax, jax.numpy as jnp
from jax import lax
from jax.experimental import pallas as pl
from jax.experimental.pallas import tpu as pltpu
from jax.sharding import PartitionSpec as P

f32, bf16 = jnp.float32, jnp.bfloat16
T, D, FF = 2048, 1024, 2560
NT, FT = 5, 512
NQ, LANES = 4, 128
MB = 512
SUBS = 1
NM = T // MB
ROWS = FF // 4
AXES = ("x", "y", "z")
STRIDE = {"x": 32, "y": 8, "z": 2}
ORDER = (("x", "y", "z"), ("y", "z", "x"), ("z", "x", "y"))
LEFT, RIGHT, ACROSS = 3, 1, 2
GU, DOWN = (0, 1), 2
CHIPS = (4, 4, 4)
BLOCK = ((8, FT), (8, FT), (40, LANES))
TILE = ((*CHIPS, 2, *BLOCK[0]), (*CHIPS, 2, *BLOCK[1]), (2, *CHIPS, *BLOCK[DOWN]))
NTILES = (NT, NT, NQ)
VMEM = (64 << 20) - (64 << 10)
ALL = slice(None)


def dot(a, b):
    return jnp.dot(a, b, preferred_element_type=f32)


def dot_t(a, b):
    return lax.dot_general(a, b, (((1,), (1,)), ((), ())), preferred_element_type=f32)


def mult(x, n):
    return x if isinstance(x, int) else pl.multiple_of(x, n)


def span(i, n):
    return pl.ds(mult(i * n, n), n)


def sigmoid(x):
    return 0.5 * jnp.tanh(0.5 * x) + 0.5


def normed(h):
    w = h.astype(f32)
    return (w * lax.rsqrt(jnp.mean(w * w, -1, keepdims=True) + 1e-6)).astype(bf16)


def norm_back(h, da, dh):
    w = h.astype(f32)
    s = lax.rsqrt(jnp.mean(w * w, -1, keepdims=True) + 1e-6)
    d = da.astype(bf16).astype(f32)
    c = jnp.sum(d * w, -1, keepdims=True) * (s * s * s / D)
    return (dh.astype(f32) + (d * s - w * c).astype(bf16).astype(f32)).astype(bf16)


class Place:
    def __init__(self):
        self.me = lax.axis_index("dp")
        self.core = self.me % 2
        self.at = {a: self.me // STRIDE[a] % 4 for a in AXES}

    def ring(self, axis, d):
        return (self.at[axis] + d) % 4

    def shifted(self, *moves):
        return {"dp": self.me + sum((self.ring(a, d) - self.at[a]) * STRIDE[a] for a, d in moves)}

    def partner(self):
        return {"dp": self.me + 1 - 2 * self.core}

    def in_plane(self, c, k, way=1):
        return tuple(zip(ORDER[c][:2], (way * (k // 4) % 4, way * (k % 4) % 4)))

    def enter(self, still):
        barrier = pltpu.get_barrier_semaphore()
        moves = [m for m in itertools.product(range(4), repeat=3) if 3 > m.count(0) >= still]
        for m in moves:
            pl.semaphore_signal(barrier, inc=1, device_id=self.shifted(*zip(AXES, m)))
        pl.semaphore_signal(barrier, inc=1, device_id=self.partner())
        pl.semaphore_wait(barrier, len(moves) + 1)


PEERS = range(1, 16)


def remote(src, dst, send, recv, to):
    return pltpu.make_async_remote_copy(src_ref=src, dst_ref=dst, send_sem=send, recv_sem=recv, device_id=to)


def block(c, place, moves=()):
    pos = dict(moves)
    return tuple(place.ring(a, pos[a]) if a in pos else place.at[a] for a in AXES)


def plane(c, r, half=None):
    o = ORDER[c]
    pos = {o[0]: ALL if half is None else pl.ds(2 * half, 2), o[1]: ALL, o[2]: r}
    return tuple(pos[a] for a in AXES)


def joint(place, buf, sem):
    return remote(buf, buf, *sem, place.partner())


class Gather:
    STAGES = 6

    def __init__(self, place, ins, outs, send, recv):
        self.p, self.ins, self.outs, self.send, self.recv = place, ins, outs, send, recv

    def own(self, c, q):
        l = (q >= NTILES[c]).astype(jnp.int32)
        t = q - l * NTILES[c]
        return l, ALL, span(t, FT) if c in GU else span(t * 2 + self.p.core, LANES)

    def at(self, c, q, i):
        return self.outs[c].at[(q, *i, self.p.core) if c in GU else (q, self.p.core, *i)]

    def line(self, c, s, r):
        o = ORDER[c]
        pos = {o[0]: ALL if s else r, o[1]: r if s else self.p.at[o[1]], o[2]: self.p.at[o[2]]}
        return tuple(pos[a] for a in AXES)

    def copies(self, s, c, q):
        p, o = self.p, ORDER[c]
        sems = (self.send.at[q, c], self.recv.at[q, c, s])
        if s < 2:
            to = self.at(c, q, self.line(c, s, p.at[o[s]]))
            return [remote(to if s else self.ins[c].at[self.own(c, q)], to, *sems, p.shifted((o[s], k))) for k in (1, 2, 3)]
        if s == 4:
            half = self.at(c, q, (ALL,) * 3)
            return [remote(half, half, *sems, p.partner())]
        if s == 2:
            whole = [self.at(c, q, plane(c, p.at[o[2]]))] * 2
        else:
            whole = [self.at(c, q, plane(c, p.ring(o[2], d), h)) for h, d in enumerate((LEFT, RIGHT))]
        return [remote(whole[h], whole[h], *sems, p.shifted((o[2], d))) for h, d in enumerate((RIGHT, LEFT))]

    def joint(self, s, c, q):
        part = self.line(c, s, pl.ds(0, 3)) if s < 2 else (plane(c, pl.ds(0, 2)), plane(c, 0), (ALL,) * 3)[s - 2]
        ref = self.at(c, q, part)
        return remote(ref, ref, self.send.at[q, c], self.recv.at[q, c, s], self.p.partner())

    def keep(self, c, q):
        b = block(c, self.p)
        self.outs[c][(q, *b, self.p.core) if c in GU else (q, self.p.core, *b)] = self.ins[c][self.own(c, q)]

    def stage(self, s, c, q):
        if s > 0:
            self.joint(s - 1, c, q).wait()
        if s < 5:
            for x in self.copies(s, c, q): x.start()


def join_down(place, w_in, peer, chip):
    first = place.core == 0
    mine, other = w_in[...].astype(f32), peer[...].astype(f32)
    chip[...] = jnp.concatenate([jnp.where(first, mine, other), jnp.where(first, other, mine)], axis=1).astype(bf16)


OFFSET = (0, 1, 1)
AHEAD = 12
NEXT = 7


def fwd_kernel(x_hbm, wg_in, wu_in, wd_in, h1_hbm, g_hbm, u_hbm, at_hbm, wg0, wu0, wd0, wg1, wu1, wd1,
               x, a, act, tg, tu, td, gb, ub, atb, peer, chip, send, recv, jsem, wsem, osem, xsem):
    place = Place()
    load_x = pltpu.make_async_copy(x_hbm, x, xsem)
    load_x.start()
    place.enter(2)
    join = remote(wd_in, peer, jsem.at[0], jsem.at[1], place.partner())
    join.start()
    gather = Gather(place, (wg_in, wu_in, chip), (tg, tu, td), send, recv)

    def tick(i):
        def stages(colors):
            for s in reversed(range(Gather.STAGES)):
                for c in colors:
                    n = i // 2 - s
                    l = (n >= NEXT).astype(jnp.int32)
                    t = n - l * NEXT
                    @pl.when((t >= 0) & (t < NTILES[c]))
                    def _():
                        gather.stage(s, c, t + l * NTILES[c])
        for odd, colors in enumerate(((0,), (1, 2))):
            @pl.when(i % 2 == odd)
            def _(): stages(colors)

    def kept(l, t):
        return [pltpu.make_async_copy(v.at[t + l * NT], o.at[t], wsem.at[l, t, c]) for c, (v, o) in enumerate((((tg, wg0), (tu, wu0)), ((tg, wg1), (tu, wu1)))[l])]
    def kept_down(l, q):
        return pltpu.make_async_copy(td.at[q + l * NQ], (wd0, wd1)[l].at[q], wsem.at[l, q, DOWN])
    def out(l, t, m, s):
        r = span(m, MB)
        return [pltpu.make_async_copy(gb.at[s], g_hbm.at[l, t, r], osem.at[0, s]),
                pltpu.make_async_copy(ub.at[s], u_hbm.at[l, t, r], osem.at[1, s]),
                pltpu.make_async_copy(atb.at[s], at_hbm.at[l, span(t, FT), r], osem.at[2, s])]

    def gate_up(l, i):
        t, m, o = i // NM, i % NM, i % 2
        @pl.when(m == 0)
        def _():
            for v in kept(l, t): v.start()
        @pl.when(i >= 2)
        def _():
            for v in out(l, t, m, o): v.wait()
        am = a[span(m, MB), :]
        g = dot(am, tg[t + l * NT].reshape(D, FT))
        u = dot(am, tu[t + l * NT].reshape(D, FT))
        gb[o] = g
        ub[o] = u
        ac = (g * sigmoid(g) * u).astype(bf16)
        if l == 0:
            act[span(m, MB), span(t, FT)] = ac
        atb[o] = ac.T
        for v in out(l, t, m, o): v.start()

    def keep_all(c):
        @pl.loop(0, 2 * NTILES[c])
        def _(q): gather.keep(c, q)

    keep_all(0)
    tick(jnp.int32(0))
    keep_all(1)
    join.wait()
    join_down(place, wd_in, peer, chip)
    keep_all(DOWN)
    load_x.wait()
    rows = 2 * LANES
    @pl.loop(1, AHEAD)
    def _(i):
        tick(i)
        @pl.when(i <= T // rows)
        def _():
            r = span(i - 1, rows)
            a[r, :] = normed(x[r, :])

    @pl.loop(0, NT * NM)
    def _(i):
        t, m = i // NM, i % NM
        @pl.when((m == 0) & (t == NT - 1))
        def _():
            for q in range(NQ): kept_down(0, q).start()
        gate_up(0, i)
        @pl.when(m % 2 == 1)
        def _():
            tick(AHEAD + i // 2)

    @pl.loop(0, NM)
    def _(m):
        r = span(m, MB)
        v = dot(act[r, :], jnp.concatenate([td[j // 2, j % 2].reshape(FF, LANES) for j in range(2 * NQ)], axis=1))
        h = (x[r, :].astype(f32) + v.astype(bf16).astype(f32)).astype(bf16)
        x[r, :] = h
        a[r, :] = normed(h)
        tick(AHEAD + 2 * NT + m)
    save_h = pltpu.make_async_copy(x, h1_hbm, xsem)
    save_h.start()
    for i in (NT * NM - 2, NT * NM - 1):
        for v in out(0, i // NM, i % NM, i % 2): v.wait()

    @pl.loop(0, NT * NM)
    def _(i):
        gate_up(1, i)
        @pl.when(i % 2 == 1)
        def _():
            tick(AHEAD + 2 * NT + NM + i // 2)
    for q in range(NQ): kept_down(1, q).start()
    for i in (NT * NM - 2, NT * NM - 1):
        for v in out(1, i // NM, i % NM, i % 2): v.wait()
    for l in range(2):
        for t in range(NT):
            for v in kept(l, t): v.wait()
        for q in range(NQ): kept_down(l, q).wait()
    save_h.wait()


VM = pl.BlockSpec(memory_space=pltpu.VMEM)
ANY = pl.BlockSpec(memory_space=pl.ANY)
DMA = pltpu.SemaphoreType.DMA


def of(dtype, *shape):
    return jax.ShapeDtypeStruct(shape, dtype)


def vm(*shape, dtype=bf16):
    return pltpu.VMEM(shape, dtype)


def forward(x, *weights):
    tiles = [of(bf16, n, *tile) for n, tile in zip(NTILES, TILE)]
    return pl.pallas_call(
        fwd_kernel, name="fwd",
        out_shape=[of(bf16, T, D), of(f32, 2, NT, T, FT), of(f32, 2, NT, T, FT), of(bf16, 2, FF, T)] + tiles * 2,
        in_specs=[ANY] + [VM] * 3, out_specs=[ANY] * 10,
        scratch_shapes=[vm(T, D), vm(T, D), vm(T, FF)] + [vm(2 * n, *tile) for n, tile in zip(NTILES, TILE)] + [
            vm(2, MB, FT, dtype=f32), vm(2, MB, FT, dtype=f32), vm(2, FT, MB), vm(2, 20, D), vm(2, 40, D),
            DMA((2 * NT, 3)), DMA((2 * NT, 3, 5)), DMA((2,)), DMA((2, NT, 3)), DMA((3, 2)), DMA],
        compiler_params=pltpu.CompilerParams(collective_id=0, has_side_effects=True, vmem_limit_bytes=VMEM),
    )(x, *weights)


class Scatter:
    STAGES = 6

    def __init__(self, place, c, slots, total, tile, out, fin, sums, halves, wholes, blocks, send, recv, credit, osem):
        self.p, self.c, self.slots, self.total, self.tile, self.out, self.fin = place, c, slots, total, tile, out, fin
        self.sums, self.halves, self.wholes, self.blocks = sums, halves, wholes, blocks
        self.send, self.recv, self.credit, self.osem = send, recv, credit, osem

    def final(self, q, core):
        n = NTILES[self.c]
        l = (q < n).astype(jnp.int32)
        t = q + (l - 1) * n
        return (l, ALL, span(t, FT) if self.c in GU else span(t * 2 + core, LANES))

    def slot(self, q):
        return q % 2 if self.c in GU else q - 3 * (q * 11 // 32)

    def sem(self, q, k):
        return self.send.at[self.slot(q), k], self.recv.at[self.slot(q), k]

    def copies(self, s, q):
        p, c, n = self.p, self.c, self.slot(q)
        sem = functools.partial(self.sem, q)
        if s == 0:
            t = self.tile(q)
            return [remote(t.at[:, :, :, 1 - p.core] if c in GU else t.at[1 - p.core], self.sums.at[n], *sem(0), p.partner())]
        if s == 3:
            ways = [(k, p.in_plane(c, k, -1)) for k in PEERS]
            return [remote(self.sums.at[(n, *block(c, p, m))], self.blocks.at[n, k - 1], *sem(5), p.shifted(*m)) for k, m in ways]
        if s == 4:
            end = self.sums.at[(n, *block(c, p))]
            if c in GU:
                return [pltpu.make_async_copy(end, self.out.at[self.final(q, 0)], self.osem.at[n])]
            return [remote(end, self.fin.at[self.final(q, p.core)], *sem(6), p.partner())]
        a = ORDER[c][2]
        ways = (RIGHT, LEFT)
        if s == 1:
            two = [(self.sums.at[(n, *plane(c, p.ring(a, ACROSS), d))], self.halves.at[n, d]) for d in (0, 1)]
        else:
            two = [(self.sums.at[(n, *plane(c, p.ring(a, ways[d])))], self.wholes.at[n, d]) for d in (0, 1)]
        return [remote(*two[d], *sem(2 * s - 1 + d), p.shifted((a, ways[d]))) for d in (0, 1)]

    def add(self, i, *terms):
        v = self.sums[i].astype(f32)
        for t in terms: v = v + t.astype(f32)
        self.sums[i] = v.astype(bf16)

    def stage(self, s, q):
        p, c, n = self.p, self.c, self.slot(q)
        a = ORDER[c][2]
        if s == 4:
            joint(p, self.blocks.at[n], self.sem(q, 5)).wait()
        elif s > 0:
            for x in self.copies(s - 1, q): x.wait()
        if s == 0:
            @pl.when(q >= self.slots)
            def _():
                for i in range(18): pl.semaphore_wait(self.credit.at[i], 1)
        elif s == 1:
            t = self.tile(q)
            @pl.loop(0, 4)
            def _(x):
                self.add((n, x), t[x, :, :, p.core] if c in GU else t[p.core, x])
        elif s == 2:
            for d, way in enumerate((RIGHT, LEFT)):
                self.add((n, *plane(c, p.ring(a, way), d)), self.halves[n, d])
        elif s == 3:
            self.add((n, *plane(c, p.at[a])), self.wholes[n, 0], self.wholes[n, 1])
        elif s == 4:
            self.add((n, *block(c, p)), *(self.blocks[n, k - 1] for k in PEERS))
        else:
            if c == DOWN:
                self.fin[self.final(q, p.core)] = self.sums[(n, *block(c, p))]
            @pl.when(q < self.total - self.slots)
            def _():
                others = [p.partner(), p.shifted((a, LEFT)), p.shifted((a, RIGHT))] + [p.shifted(*p.in_plane(c, k)) for k in PEERS]
                for i, other in enumerate(others):
                    pl.semaphore_signal(self.credit.at[i], inc=1, device_id=other)
        if s < 5:
            for x in self.copies(s, q): x.start()


SLOTS = (2, 2, 3)
STEP = 6
FIRST, LATER = (1, 3, 5), (2, 4)
EVERY, DOWN_AT = 3, (0, 1, 3, 5, 7, 8)
DOWN1, DOWN0, LAST = 5, 8, 12


def bwd_kernel(h_hbm, dy_hbm, x_hbm, g_hbm, u_hbm, at_hbm, wg0, wu0, wd0, wg1, wu1, wd1,
               dx_hbm, og, ou, od,
               a, dh, at, acc, dg, du, wg, wu, wd, ob, dob, actt, gb, ub,
               wsem, gsem, dsem, xsem, *refs):
    place = Place()
    place.enter(1)
    refs = list(refs)
    take = lambda n: [refs.pop(0) for _ in range(n)]
    fin, = take(1)
    tiles = (lambda q: ob.at[q % 2, 0], lambda q: ob.at[q % 2, 1], lambda q: dob.at[q % NQ])
    outs = (og, ou, None)
    sc = []
    for c in range(3):
        sc.append(Scatter(place, c, SLOTS[c], 2 * NTILES[c], tiles[c], outs[c], fin, *take(8)))

    def weights(f, s):
        for l, (g_, u_, d_) in enumerate(((wg1, wu1, wd1), (wg0, wu0, wd0))):
            t = f - l * NT
            yield (t >= 0) & (t < NT), [pltpu.make_async_copy(g_.at[t], wg.at[s], wsem.at[0, s]), pltpu.make_async_copy(u_.at[t], wu.at[s], wsem.at[1, s])] + [
                pltpu.make_async_copy(d_.at[j // 2, j % 2, span(t, FT)], wd.at[s, :, span(j, LANES)], wsem.at[2 + j, s]) for j in range(2 * NQ)]
    def saved(i, s):
        l = (i < NT * NM).astype(jnp.int32)
        at = (l, i // NM + (l - 1) * NT, span(i % NM, MB))
        return [pltpu.make_async_copy(g_hbm.at[at], gb.at[s], gsem.at[0, s]), pltpu.make_async_copy(u_hbm.at[at], ub.at[s], gsem.at[1, s])]
    def act_in(l, t):
        return pltpu.make_async_copy(at_hbm.at[l, span(t, ROWS)], actt.at[t % 2], dsem.at[t % 2])
    def dx_out(m):
        return pltpu.make_async_copy(dh.at[span(m, MB)], dx_hbm.at[span(m, MB)], xsem.at[m])

    load_h, load_dy, load_x = (pltpu.make_async_copy(src, dst, xsem.at[i]) for i, (src, dst) in enumerate(((h_hbm, a), (dy_hbm, dh), (x_hbm, a))))
    loads = (load_h, load_dy)
    for x in loads: x.start()
    zero = jnp.int32(0)
    for x in next(weights(zero, 0))[1] + saved(zero, 0): x.start()
    for x in loads: x.wait()

    rows = 256
    @pl.loop(0, T // rows)
    def _(i):
        at[:, span(i, rows)] = normed(a[span(i, rows), :]).T

    def ff_block(f, s, m):
        r, o, i = span(m, MB), m % 2, f * NM + m
        for x in saved(i, o): x.wait()
        @pl.when(i + 1 < 2 * NT * NM)
        def _():
            for x in saved(i + 1, 1 - o): x.start()
        g, u = gb[o], ub[o]
        d = dot_t(dh[r, :], wd[s]).astype(bf16).astype(f32)
        sg = sigmoid(g)
        p = g * sg
        dgv = (d * u * (sg + p * (1 - sg))).astype(bf16)
        duv = (d * p).astype(bf16)
        dg[r, :] = dgv
        du[r, :] = duv
        acc[r, :] += dot_t(dgv, wg[s].reshape(D, FT)) + dot_t(duv, wu[s].reshape(D, FT))

    def tick(S, j):
        def gate_up(s, back):
            S0 = S - back
            @pl.when((S0 >= 0) & (S0 < LAST) & (S0 != DOWN1) & (S0 != DOWN0))
            def _():
                q = S0 - (S0 > DOWN1).astype(jnp.int32) - (S0 > DOWN0).astype(jnp.int32)
                for c in GU: sc[c].stage(s, q)
        for k, i in enumerate(LATER):
            if j == i: gate_up(1 + len(FIRST) + k, 2)
        for k, i in enumerate(FIRST):
            if j == i: gate_up(1 + k, 1)
        if j == STEP - 1: gate_up(0, 0)
        @pl.when(S > DOWN1)
        def _():
            for s in reversed(range(Scatter.STAGES)):
                if (j - DOWN_AT[s]) % EVERY == 0:
                    l = (S > DOWN0).astype(jnp.int32)
                    d = STEP // EVERY * (S - (DOWN1 + 1) - l * (DOWN0 - DOWN1)) + (j - DOWN_AT[s]) // EVERY
                    @pl.when((d >= 0) & (d < NQ))
                    def _(): sc[DOWN].stage(s, d + NQ * l)

    def block_of(S, j):
        is_down = (S == DOWN1) | (S == DOWN0)
        is_ff = (S < LAST) & (S != DOWN1) & (S != DOWN0)
        f = S - (S > DOWN1).astype(jnp.int32) - (S > DOWN0).astype(jnp.int32)
        s = f % 2
        @pl.when(is_ff & (j == 0))
        def _():
            @pl.when((f == 0) | (f == NT))
            def _():
                acc[...] = jnp.zeros_like(acc)
            for ok, copies in weights(f, s):
                @pl.when(ok)
                def _():
                    for x in copies: x.wait()
        @pl.when(is_ff & (j == STEP - 1))
        def _():
            for ok, copies in weights(f + 1, 1 - s):
                @pl.when(ok & (f + 1 < 2 * NT))
                def _():
                    for x in copies: x.start()
        @pl.when(is_ff & (j < NM))
        def _():
            ff_block(f, s, j)
        @pl.when(is_ff & (j >= NM))
        def _():
            r, x = span(j - NM, MB), pl.ds(2 * (j - NM), 2)
            for c, v in ((0, dg), (1, du)):
                ob[s, c, x] = dot(at[r, :], v[...]).reshape(2, *TILE[c][1:]).astype(bf16)
        @pl.when(is_down)
        def _():
            l = (S == DOWN1).astype(jnp.int32)
            @pl.when(j == 0)
            def _():
                act_in(l, 0).start()
                @pl.when(S == DOWN1)
                def _(): load_h.start()
            @pl.when(j < 4)
            def _():
                act_in(l, j).wait()
                @pl.when(j < 3)
                def _(): act_in(l, j + 1).start()
                v = dot(actt[j % 2], dh[...])
                for k in range(2 * NQ):
                    dob[k // 2, k % 2, j] = v[:, k * LANES:(k + 1) * LANES].reshape(4, 4, 40, LANES).astype(bf16)
            @pl.when((S == DOWN1) & (j == NT))
            def _():
                load_h.wait()
                @pl.loop(0, T // rows)
                def _(i):
                    r = span(i, rows)
                    dh[r, :] = norm_back(a[r, :], acc[r, :], dh[r, :])
                load_x.start()
                load_x.wait()
                @pl.loop(0, T // rows)
                def _(i):
                    at[:, span(i, rows)] = normed(a[span(i, rows), :]).T
        @pl.when((S == LAST) & (j < NM))
        def _():
            r = span(j, MB)
            dh[r, :] = norm_back(a[r, :], acc[r, :], dh[r, :])
            dx_out(j).start()
        for k in range(STEP):
            @pl.when(j == k)
            def _(): tick(S, k)
    @pl.loop(0, LAST + 2)
    def _(S):
        @pl.loop(0, STEP)
        def _(j): block_of(S, j)

    first = place.core == 0
    v = fin[...].astype(f32)
    od[...] = jnp.where(first, v[:, :20], v[:, 20:]).astype(bf16)
    for m in range(NM): dx_out(m).wait()


def backward(h1, dy, x, g, u, at, *tiles):
    tiles = [t if i % 3 in GU else t.reshape(NQ, 2, FF, LANES) for i, t in enumerate(tiles)]
    rings = []
    for c in range(3):
        n = SLOTS[c]
        flat = [4 // (1 + (ORDER[c][0] == x)) for x in AXES if x != ORDER[c][2]]
        rings += [vm(n, *CHIPS, *BLOCK[c]), vm(n, 2, *flat, *BLOCK[c]), vm(n, 2, 4, 4, *BLOCK[c]), vm(n, 15, *BLOCK[c]),
                  DMA((n, 7)), DMA((n, 7)), pltpu.SemaphoreType.REGULAR((18,)), DMA((n,))]
    return pl.pallas_call(
        bwd_kernel, name="bwd",
        out_shape=[of(bf16, T, D), of(bf16, 2, 8, FF), of(bf16, 2, 8, FF), of(bf16, 2, 20, D)],
        in_specs=[ANY] * 12, out_specs=[ANY] * 3 + [VM],
        scratch_shapes=[vm(T, D), vm(T, D), vm(D, T), vm(T, D, dtype=f32), vm(T, FT), vm(T, FT), vm(2, *TILE[0]), vm(2, *TILE[1]), vm(2, FT, D),
                        vm(2, 2, *TILE[0]), vm(NQ, *TILE[DOWN]), vm(2, ROWS, T), vm(2, MB, FT, dtype=f32), vm(2, MB, FT, dtype=f32),
                        DMA((10, 2)), DMA((2, 2)), DMA((2,)), DMA((NM,)), vm(2, 40, D)] + rings,
        compiler_params=pltpu.CompilerParams(collective_id=1, has_side_effects=True, vmem_limit_bytes=VMEM),
    )(h1, dy, x, g, u, at, *tiles)


def solution(mesh):
    def step(x, dy, *weights):
        h1, *saved = forward(x[0], *weights)
        dx, *grads = backward(h1, dy[0], x[0], *saved)
        return (dx[None], *grads)

    tokens, rows = P(("rep", "dp")), P(None, "dp", None)
    return jax.shard_map(step, mesh=mesh, in_specs=(tokens, tokens, rows, rows, rows), out_specs=(tokens,) + (P("rep", "dp", None),) * 3, check_vma=False)
```

time: 375 us -> 354 us (0.944)
  Pallas kernels: 365 us -> 344 us
    pallas_call x1, Pallas kernels: 254 us -> 227 us  [backward(): pl.pallas_call(bwd_kernel, name='bwd', out_shape=[of(bf16, T, D), of(bf16...]
    pallas_call x1, Pallas kernels: 111 us -> 118 us  [forward(): pl.pallas_call(fwd_kernel, name='fwd', out_shape=[of(bf16, T, D), of(f32,...]
where the time goes in v4:
time: 354 us
  Pallas kernels  344 us (97%)
  local copies, waits for them, and re-layouts  9.11 us (3%)
    pallas_call x1, Pallas kernels, backward(): pl.pallas_call(bwd_kernel, name='bwd', out_shape=[of(bf16, T, D), of(bf16...  227 us
    pallas_call x1, Pallas kernels, forward(): pl.pallas_call(fwd_kernel, name='fwd', out_shape=[of(bf16, T, D), of(f32,...  118 us
    unnamed x9, local copies, waits for them, and re-layouts  9.11 us

profile of v4, /device:TPU:0, one launch (start us, length us, event | category | flops | bytes accessed | tf_op | source)
XLA Modules:
  0.0 353.9 jit_solution(6222625909460870059)
XLA Ops:
  0.6 1.5 copy.9.wd_in
  2.2 117.5 %fwd.1 = (bf16[2048,1024]{1,0:T(8,128)(2,1)}, f32[2,5,2048,512]{3,2,1,0:T(8,128)}, f32[2,5,2048,512]{3,2,1,0:T(8,128)}, bf16[2,2560,2048]{2,1,0:T(8,128)(2,1)}, ...) custom-call(bf16[2048,1024]{1,0:T(8,128)(2,1)} %bitcast.5, ...), custom_call_target="tpu_custom_call" | custom-call | tf_op jit(solution)/shard_map/fwd/pallas_call | solution.py:300
  119.7 226.6 %bwd.1 = (bf16[2048,1024]{1,0:T(8,128)(2,1)}, bf16[2,8,2560]{2,1,0:T(8,128)(2,1)}, bf16[2,8,2560]{2,1,0:T(8,128)(2,1)}, bf16[2,20,1024]{2,1,0:T(8,128)(2,1)}) custom-call(bf16[2048,1024]{1,0:T(8,128)(2,1)} %get-tuple-element.18.h_hbm, bf16[2048,1024]{1,0:T(8,128)(2,1)} %bitcast.9, bf16[2048,1024]{1,0:T(8,128)(2,1)} %bitcast.6, ...), custom_call_target="tpu_custom_call" | custom-call | tf_op jit(solution)/shard_map/bwd/pallas_call | solution.py:561
  346.3 0.0 copy-start.1
  346.3 0.0 copy-start
  346.3 1.6 copy.10
  348.0 4.6 %copy.14 = bf16[1,2048,1024]{2,1,0:T(8,128)(2,1)} copy(bf16[1,2048,1024]{2,1,0:T(8,128)(2,1)} %bitcast.10) | data formatting | bytes 8388608
  352.6 0.0 copy-done.1
  352.6 0.6 copy.15
  353.3 0.0 copy-done
  353.3 0.6 copy.16
Async XLA Ops:
  346.3 6.3 %copy-start.1 = (bf16[2,8,2560]{2,1,0:T(8,128)(2,1)S(1)}, bf16[2,8,2560]{2,1,0:T(8,128)(2,1)}, u32[]{:S(2)}) copy-start(bf16[2,8,2560]{2,1,0:T(8,128)(2,1)} %get-tuple-element.41) | copy-start | bytes 245764
  346.3 6.9 %copy-start = (bf16[2,8,2560]{2,1,0:T(8,128)(2,1)S(1)}, bf16[2,8,2560]{2,1,0:T(8,128)(2,1)}, u32[]{:S(2)}) copy-start(bf16[2,8,2560]{2,1,0:T(8,128)(2,1)} %get-tuple-element.42) | copy-start | bytes 245764

commit v5 on v4

--- a/solution.py
+++ b/solution.py
@@ -160,8 +160,9 @@
 
 def join_down(place, w_in, peer, chip):
     first = place.core == 0
-    mine, other = w_in[...].astype(f32), peer[...].astype(f32)
-    chip[...] = jnp.concatenate([jnp.where(first, mine, other), jnp.where(first, other, mine)], axis=1).astype(bf16)
+    for l in range(2):
+        mine, other = w_in[:, l, :].astype(f32), peer[:, l, :].astype(f32)
+        chip[l] = jnp.concatenate([jnp.where(first, mine, other), jnp.where(first, other, mine)], axis=0).astype(bf16)
 
 
 OFFSET = (0, 1, 1)
@@ -169,8 +170,8 @@
 NEXT = 7
 
 
-def fwd_kernel(x_hbm, wg_in, wu_in, wd_in, h1_hbm, g_hbm, u_hbm, at_hbm, wg0, wu0, wd0, wg1, wu1, wd1,
-               x, a, act, tg, tu, td, gb, ub, atb, peer, chip, send, recv, jsem, wsem, osem, xsem):
+def fwd_kernel(x_hbm, wg_in, wu_in, wd_in, h1_hbm, na_hbm, g_hbm, u_hbm, at_hbm, wg0, wu0, wd0, wg1, wu1, wd1,
+               x, a, act, tg, tu, td, gb, ub, atb, nab, peer, chip, send, recv, jsem, wsem, osem, xsem, nsem):
     place = Place()
     load_x = pltpu.make_async_copy(x_hbm, x, xsem)
     load_x.start()
@@ -234,13 +235,21 @@
     keep_all(DOWN)
     load_x.wait()
     rows = 2 * LANES
+    def normed_out(l, i):
+        return pltpu.make_async_copy(nab.at[i % 2], na_hbm.at[l, :, span(i, rows)], nsem.at[i % 2])
+    def keep_normed(l, i):
+        v = normed(x[span(i, rows), :])
+        a[span(i, rows), :] = v
+        @pl.when(i >= 2)
+        def _(): normed_out(l, i).wait()
+        nab[i % 2] = v.T
+        normed_out(l, i).start()
     @pl.loop(1, AHEAD)
     def _(i):
         tick(i)
         @pl.when(i <= T // rows)
-        def _():
-            r = span(i - 1, rows)
-            a[r, :] = normed(x[r, :])
+        def _(): keep_normed(0, i - 1)
+    for i in range(2): normed_out(0, i).wait()
 
     @pl.loop(0, NT * NM)
     def _(i):
@@ -259,8 +268,9 @@
         v = dot(act[r, :], jnp.concatenate([td[j // 2, j % 2].reshape(FF, LANES) for j in range(2 * NQ)], axis=1))
         h = (x[r, :].astype(f32) + v.astype(bf16).astype(f32)).astype(bf16)
         x[r, :] = h
-        a[r, :] = normed(h)
+        for k in range(2): keep_normed(1, 2 * m + k)
         tick(AHEAD + 2 * NT + m)
+    for i in range(2): normed_out(1, i).wait()
     save_h = pltpu.make_async_copy(x, h1_hbm, xsem)
     save_h.start()
     for i in (NT * NM - 2, NT * NM - 1):
@@ -299,11 +309,11 @@
     tiles = [of(bf16, n, *tile) for n, tile in zip(NTILES, TILE)]
     return pl.pallas_call(
         fwd_kernel, name="fwd",
-        out_shape=[of(bf16, T, D), of(f32, 2, NT, T, FT), of(f32, 2, NT, T, FT), of(bf16, 2, FF, T)] + tiles * 2,
-        in_specs=[ANY] + [VM] * 3, out_specs=[ANY] * 10,
+        out_shape=[of(bf16, T, D), of(bf16, 2, D, T), of(f32, 2, NT, T, FT), of(f32, 2, NT, T, FT), of(bf16, 2, FF, T)] + tiles * 2,
+        in_specs=[ANY] + [VM] * 3, out_specs=[ANY] * 11,
         scratch_shapes=[vm(T, D), vm(T, D), vm(T, FF)] + [vm(2 * n, *tile) for n, tile in zip(NTILES, TILE)] + [
-            vm(2, MB, FT, dtype=f32), vm(2, MB, FT, dtype=f32), vm(2, FT, MB), vm(2, 20, D), vm(2, 40, D),
-            DMA((2 * NT, 3)), DMA((2 * NT, 3, 5)), DMA((2,)), DMA((2, NT, 3)), DMA((3, 2)), DMA],
+            vm(2, MB, FT, dtype=f32), vm(2, MB, FT, dtype=f32), vm(2, FT, MB), vm(2, D, 2 * LANES), vm(20, 2, D), vm(2, 40, D),
+            DMA((2 * NT, 3)), DMA((2 * NT, 3, 5)), DMA((2,)), DMA((2, NT, 3)), DMA((3, 2)), DMA, DMA((2,))],
         compiler_params=pltpu.CompilerParams(collective_id=0, has_side_effects=True, vmem_limit_bytes=VMEM),
     )(x, *weights)
 
@@ -323,7 +333,7 @@
         return (l, ALL, span(t, FT) if self.c in GU else span(t * 2 + core, LANES))
 
     def slot(self, q):
-        return q % 2 if self.c in GU else q - 3 * (q * 11 // 32)
+        return q % self.slots
 
     def sem(self, q, k):
         return self.send.at[self.slot(q), k], self.recv.at[self.slot(q), k]
@@ -390,14 +400,14 @@
             for x in self.copies(s, q): x.start()
 
 
-SLOTS = (2, 2, 3)
+SLOTS = (2, 2, 4)
 STEP = 6
-FIRST, LATER = (1, 3, 5), (2, 4)
-EVERY, DOWN_AT = 3, (0, 1, 3, 5, 7, 8)
+FIRST, LATER = (1, 3), (0, 3, 4)
+EVERY, DOWN_AT = 3, (0, 1, 4, 7, 10, 11)
 DOWN1, DOWN0, LAST = 5, 8, 12
 
 
-def bwd_kernel(h_hbm, dy_hbm, x_hbm, g_hbm, u_hbm, at_hbm, wg0, wu0, wd0, wg1, wu1, wd1,
+def bwd_kernel(h_hbm, na_hbm, dy_hbm, x_hbm, g_hbm, u_hbm, at_hbm, wg0, wu0, wd0, wg1, wu1, wd1,
                dx_hbm, og, ou, od,
                a, dh, at, acc, dg, du, wg, wu, wd, ob, dob, actt, gb, ub,
                wsem, gsem, dsem, xsem, *refs):
@@ -427,17 +437,14 @@
         return pltpu.make_async_copy(dh.at[span(m, MB)], dx_hbm.at[span(m, MB)], xsem.at[m])
 
     load_h, load_dy, load_x = (pltpu.make_async_copy(src, dst, xsem.at[i]) for i, (src, dst) in enumerate(((h_hbm, a), (dy_hbm, dh), (x_hbm, a))))
-    loads = (load_h, load_dy)
+    load_at = [pltpu.make_async_copy(na_hbm.at[l], at, xsem.at[NM - 1]) for l in range(2)]
+    loads = (load_at[1], load_dy)
     for x in loads: x.start()
     zero = jnp.int32(0)
     for x in next(weights(zero, 0))[1] + saved(zero, 0): x.start()
     for x in loads: x.wait()
 
-    rows = 256
-    @pl.loop(0, T // rows)
-    def _(i):
-        at[:, span(i, rows)] = normed(a[span(i, rows), :]).T
-
+    rows = 2 * LANES
     def ff_block(f, s, m):
         r, o, i = span(m, MB), m % 2, f * NM + m
         for x in saved(i, o): x.wait()
@@ -470,10 +477,11 @@
         def _():
             for s in reversed(range(Scatter.STAGES)):
                 if (j - DOWN_AT[s]) % EVERY == 0:
-                    l = (S > DOWN0).astype(jnp.int32)
-                    d = STEP // EVERY * (S - (DOWN1 + 1) - l * (DOWN0 - DOWN1)) + (j - DOWN_AT[s]) // EVERY
-                    @pl.when((d >= 0) & (d < NQ))
-                    def _(): sc[DOWN].stage(s, d + NQ * l)
+                    d = STEP // EVERY * (S - (DOWN1 + 1)) + (j - DOWN_AT[s]) // EVERY
+                    gap = STEP // EVERY * (DOWN0 - DOWN1) - NQ
+                    l = (d >= NQ + gap).astype(jnp.int32)
+                    @pl.when((d >= 0) & (d < 2 * NQ + gap) & ((d < NQ) | (l > 0)))
+                    def _(): sc[DOWN].stage(s, d - gap * l)
 
     def block_of(S, j):
         is_down = (S == DOWN1) | (S == DOWN0)
@@ -510,7 +518,9 @@
             def _():
                 act_in(l, 0).start()
                 @pl.when(S == DOWN1)
-                def _(): load_h.start()
+                def _():
+                    load_h.start()
+                    load_at[0].start()
             @pl.when(j < 4)
             def _():
                 act_in(l, j).wait()
@@ -527,10 +537,10 @@
                     r = span(i, rows)
                     dh[r, :] = norm_back(a[r, :], acc[r, :], dh[r, :])
                 load_x.start()
-                load_x.wait()
-                @pl.loop(0, T // rows)
-                def _(i):
-                    at[:, span(i, rows)] = normed(a[span(i, rows), :]).T
+                load_at[0].wait()
+        @pl.when((S == LAST) & (j == 0))
+        def _():
+            load_x.wait()
         @pl.when((S == LAST) & (j < NM))
         def _():
             r = span(j, MB)
@@ -545,12 +555,13 @@
         def _(j): block_of(S, j)
 
     first = place.core == 0
-    v = fin[...].astype(f32)
-    od[...] = jnp.where(first, v[:, :20], v[:, 20:]).astype(bf16)
+    for l in range(2):
+        v = fin[l].astype(f32)
+        od[:, l, :] = jnp.where(first, v[:20], v[20:]).astype(bf16)
     for m in range(NM): dx_out(m).wait()
 
 
-def backward(h1, dy, x, g, u, at, *tiles):
+def backward(h1, normed_t, dy, x, g, u, at, *tiles):
     tiles = [t if i % 3 in GU else t.reshape(NQ, 2, FF, LANES) for i, t in enumerate(tiles)]
     rings = []
     for c in range(3):
@@ -560,19 +571,21 @@
                   DMA((n, 7)), DMA((n, 7)), pltpu.SemaphoreType.REGULAR((18,)), DMA((n,))]
     return pl.pallas_call(
         bwd_kernel, name="bwd",
-        out_shape=[of(bf16, T, D), of(bf16, 2, 8, FF), of(bf16, 2, 8, FF), of(bf16, 2, 20, D)],
-        in_specs=[ANY] * 12, out_specs=[ANY] * 3 + [VM],
+        out_shape=[of(bf16, T, D), of(bf16, 2, 8, FF), of(bf16, 2, 8, FF), of(bf16, 20, 2, D)],
+        in_specs=[ANY] * 13, out_specs=[ANY] * 3 + [VM],
         scratch_shapes=[vm(T, D), vm(T, D), vm(D, T), vm(T, D, dtype=f32), vm(T, FT), vm(T, FT), vm(2, *TILE[0]), vm(2, *TILE[1]), vm(2, FT, D),
                         vm(2, 2, *TILE[0]), vm(NQ, *TILE[DOWN]), vm(2, ROWS, T), vm(2, MB, FT, dtype=f32), vm(2, MB, FT, dtype=f32),
                         DMA((10, 2)), DMA((2, 2)), DMA((2,)), DMA((NM,)), vm(2, 40, D)] + rings,
         compiler_params=pltpu.CompilerParams(collective_id=1, has_side_effects=True, vmem_limit_bytes=VMEM),
-    )(h1, dy, x, g, u, at, *tiles)
+    )(h1, normed_t, dy, x, g, u, at, *tiles)
 
 
 def solution(mesh):
     def step(x, dy, *weights):
-        h1, *saved = forward(x[0], *weights)
-        dx, *grads = backward(h1, dy[0], x[0], *saved)
+        *gate_up, down = weights
+        h1, normed_t, *saved = forward(x[0], *gate_up, down.swapaxes(0, 1))
+        dx, *grads, by_down = backward(h1, normed_t, dy[0], x[0], *saved)
+        grads.append(by_down.swapaxes(0, 1))
         return (dx[None], *grads)
 
     tokens, rows = P(("rep", "dp")), P(None, "dp", None)

time: 354 us -> 343 us (0.969)
  Pallas kernels: 344 us -> 336 us
    pallas_call x1, Pallas kernels: 227 us -> 216 us  [backward(): pl.pallas_call(bwd_kernel, name='bwd', out_shape=[of(bf16, T, D), of(bf16...]
    unnamed x9 -> x10, local copies, waits for them, and re-layouts: 9.11 us -> 6.6 us
where the time goes in v5:
time: 343 us
  Pallas kernels  336 us (98%)
  local copies, waits for them, and re-layouts  6.6 us (2%)
    pallas_call x1, Pallas kernels, backward(): pl.pallas_call(bwd_kernel, name='bwd', out_shape=[of(bf16, T, D), of(bf16...  216 us
    pallas_call x1, Pallas kernels, forward(): pl.pallas_call(fwd_kernel, name='fwd', out_shape=[of(bf16, T, D), of(bf16...  119 us

profile of v5, /device:TPU:0, one launch (start us, length us, event | category | flops | bytes accessed | tf_op | source)
XLA Modules:
  0.0 343.0 jit_solution(340591523729486488)
XLA Ops:
  0.6 119.5 %fwd.1 = (bf16[2048,1024]{1,0:T(8,128)(2,1)}, bf16[2,1024,2048]{2,1,0:T(8,128)(2,1)}, f32[2,5,2048,512]{3,2,1,0:T(8,128)}, f32[2,5,2048,512]{3,2,1,0:T(8,128)}, ...) custom-call(bf16[2048,1024]{1,0:T(8,128)(2,1)} %bitcast.7, ...), custom_call_target="tpu_custom_call" | custom-call | tf_op jit(solution)/shard_map/fwd/pallas_call | solution.py:310
  120.1 216.2 %bwd.1 = (bf16[2048,1024]{1,0:T(8,128)(2,1)}, bf16[2,8,2560]{2,1,0:T(8,128)(2,1)}, bf16[2,8,2560]{2,1,0:T(8,128)(2,1)}, bf16[20,2,1024]{2,1,0:T(2,128)(2,1)}) custom-call(bf16[2048,1024]{1,0:T(8,128)(2,1)} %get-tuple-element.19.h_hbm, bf16[2,1024,2048]{2,1,0:T(8,128)(2,1)} %get-tuple-element.20.na_hbm, bf16[2048,1024]{1,0:T(8,128)(2,1)} %bitcast.11, ...), custom_call_target="tpu_custom_call" | custom-call | tf_op jit(solution)/shard_map/bwd/pallas_call | solution.py:572
  336.3 0.0 copy-start.2
  336.4 0.0 copy-start.1
  336.4 0.0 copy-start
  336.4 4.7 %copy.13 = bf16[1,2048,1024]{2,1,0:T(8,128)(2,1)} copy(bf16[1,2048,1024]{2,1,0:T(8,128)(2,1)} %bitcast.12) | data formatting | bytes 8388608
  341.1 0.0 copy-done.2
  341.1 0.6 copy.14
  341.7 0.0 copy-done.1
  341.7 0.6 copy.15
  342.3 0.0 copy-done
  342.3 0.6 copy.16
Async XLA Ops:
  336.3 4.7 %copy-start.2 = (bf16[2,8,2560]{2,1,0:T(8,128)(2,1)S(1)}, bf16[2,8,2560]{2,1,0:T(8,128)(2,1)}, u32[]{:S(2)}) copy-start(bf16[2,8,2560]{2,1,0:T(8,128)(2,1)} %get-tuple-element.39) | copy-start | bytes 245764
  336.4 5.3 %copy-start.1 = (bf16[2,8,2560]{2,1,0:T(8,128)(2,1)S(1)}, bf16[2,8,2560]{2,1,0:T(8,128)(2,1)}, u32[]{:S(2)}) copy-start(bf16[2,8,2560]{2,1,0:T(8,128)(2,1)} %get-tuple-element.40) | copy-start | bytes 245764
  336.4 6.0 %copy-start = (bf16[20,2,1024]{2,1,0:T(2,128)(2,1)S(1)}, bf16[20,2,1024]{2,1,0:T(2,128)(2,1)}, u32[]{:S(2)}) copy-start(bf16[20,2,1024]{2,1,0:T(2,128)(2,1)} %get-tuple-element.33) | copy-start | bytes 245764

commit v6 on v5

--- a/solution.py
+++ b/solution.py
@@ -165,8 +165,7 @@
         chip[l] = jnp.concatenate([jnp.where(first, mine, other), jnp.where(first, other, mine)], axis=0).astype(bf16)
 
 
-OFFSET = (0, 1, 1)
-AHEAD = 12
+AHEAD = 11
 NEXT = 7
 
 
@@ -190,7 +189,7 @@
                     @pl.when((t >= 0) & (t < NTILES[c]))
                     def _():
                         gather.stage(s, c, t + l * NTILES[c])
-        for odd, colors in enumerate(((0,), (1, 2))):
+        for odd, colors in enumerate(((0, 1), (2,))):
             @pl.when(i % 2 == odd)
             def _(): stages(colors)
 

time: 343 us -> 340 us (level)
  Pallas kernels: 336 us -> 332 us
where the time goes in v6:
time: 340 us
  Pallas kernels  332 us (98%)
  local copies, waits for them, and re-layouts  6.6 us (2%)
    pallas_call x1, Pallas kernels, backward(): pl.pallas_call(bwd_kernel, name='bwd', out_shape=[of(bf16, T, D), of(bf16...  216 us
    pallas_call x1, Pallas kernels, forward(): pl.pallas_call(fwd_kernel, name='fwd', out_shape=[of(bf16, T, D), of(bf16...  116 us

profile of v6, /device:TPU:0, one launch (start us, length us, event | category | flops | bytes accessed | tf_op | source)
XLA Modules:
  0.0 339.6 jit_solution(11471226070786658447)
XLA Ops:
  0.6 116.1 %fwd.1 = (bf16[2048,1024]{1,0:T(8,128)(2,1)}, bf16[2,1024,2048]{2,1,0:T(8,128)(2,1)}, f32[2,5,2048,512]{3,2,1,0:T(8,128)}, f32[2,5,2048,512]{3,2,1,0:T(8,128)}, ...) custom-call(bf16[2048,1024]{1,0:T(8,128)(2,1)} %bitcast.7, ...), custom_call_target="tpu_custom_call" | custom-call | tf_op jit(solution)/shard_map/fwd/pallas_call | solution.py:309
  116.8 216.2 %bwd.1 = (bf16[2048,1024]{1,0:T(8,128)(2,1)}, bf16[2,8,2560]{2,1,0:T(8,128)(2,1)}, bf16[2,8,2560]{2,1,0:T(8,128)(2,1)}, bf16[20,2,1024]{2,1,0:T(2,128)(2,1)}) custom-call(bf16[2048,1024]{1,0:T(8,128)(2,1)} %get-tuple-element.19.h_hbm, bf16[2,1024,2048]{2,1,0:T(8,128)(2,1)} %get-tuple-element.20.na_hbm, bf16[2048,1024]{1,0:T(8,128)(2,1)} %bitcast.11, ...), custom_call_target="tpu_custom_call" | custom-call | tf_op jit(solution)/shard_map/bwd/pallas_call | solution.py:571
  332.9 0.0 copy-start.2
  332.9 0.0 copy-start.1
  333.0 0.0 copy-start
  333.0 4.7 %copy.13 = bf16[1,2048,1024]{2,1,0:T(8,128)(2,1)} copy(bf16[1,2048,1024]{2,1,0:T(8,128)(2,1)} %bitcast.12) | data formatting | bytes 8388608
  337.6 0.0 copy-done.2
  337.6 0.6 copy.14
  338.3 0.0 copy-done.1
  338.3 0.6 copy.15
  338.9 0.0 copy-done
  338.9 0.6 copy.16
Async XLA Ops:
  332.9 4.7 %copy-start.2 = (bf16[2,8,2560]{2,1,0:T(8,128)(2,1)S(1)}, bf16[2,8,2560]{2,1,0:T(8,128)(2,1)}, u32[]{:S(2)}) copy-start(bf16[2,8,2560]{2,1,0:T(8,128)(2,1)} %get-tuple-element.39) | copy-start | bytes 245764
  332.9 5.3 %copy-start.1 = (bf16[2,8,2560]{2,1,0:T(8,128)(2,1)S(1)}, bf16[2,8,2560]{2,1,0:T(8,128)(2,1)}, u32[]{:S(2)}) copy-start(bf16[2,8,2560]{2,1,0:T(8,128)(2,1)} %get-tuple-element.40) | copy-start | bytes 245764
  333.0 6.0 %copy-start = (bf16[20,2,1024]{2,1,0:T(2,128)(2,1)S(1)}, bf16[20,2,1024]{2,1,0:T(2,128)(2,1)}, u32[]{:S(2)}) copy-start(bf16[20,2,1024]{2,1,0:T(2,128)(2,1)} %get-tuple-element.33) | copy-start | bytes 245764
